TPU v7x, 16 devices: a whole 2x2x2 slice. The times are simulated.
16 devices in a mesh: tp: 2 (over z), fsdp: 8 (over y, x, core).
Axes of the slice: x: 2, y: 2, z: 2, core: 2. Of those that a mesh axis runs over, the one named last changes fastest.
Arguments:
- x: bfloat16 [16, 512, 2048], P('fsdp')
- grad_y: bfloat16 [16, 512, 2048], P('fsdp')
- w_qkv: bfloat16 [2048, 3, 16, 128], P('fsdp', None, 'tp')
- w_out: bfloat16 [16, 128, 2048], P('tp', None, 'fsdp')
- w_ff: bfloat16 [2048, 2, 8192], P('fsdp', None, 'tp')
- w_down: bfloat16 [8192, 2048], P('tp', 'fsdp')
Outputs:
- output 1: bfloat16 [16, 512, 2048], P('fsdp')
- output 2: bfloat16 [16, 512, 2048], P('fsdp')
- output 3: float32 [2048, 3, 16, 128], P('fsdp', None, 'tp')
- output 4: float32 [16, 128, 2048], P('tp', None, 'fsdp')
- output 5: float32 [2048, 2, 8192], P('fsdp', None, 'tp')
- output 6: float32 [8192, 2048], P('tp', 'fsdp')
All inputs are finite; a program needn't handle non-finite values.
Results may differ from a plain program's by a relative error of at most 0.0163043.
Values are sent between devices in bfloat16 or wider.
A program may use at most 1 GiB of HBM per device.

v0:
```python
import jax
import jax.numpy as jnp
from jax import lax
from jax.sharding import PartitionSpec as P


def layer_norm(values):
    mean_val = jnp.mean(values, axis=-1, keepdims=True)
    centered = values - mean_val
    inv_std = lax.rsqrt(jnp.mean(centered * centered, axis=-1, keepdims=True) + 1e-5)
    return centered * inv_std, inv_std


def norm_backward(grad_norm, normed, inv_std):
    grad_mean = jnp.mean(grad_norm, axis=-1, keepdims=True)
    proj_mean = jnp.mean(grad_norm * normed, axis=-1, keepdims=True)
    return inv_std * (grad_norm - grad_mean - normed * proj_mean)


def rope_tables(seq_len, head_dim):
    inv_freq = 10000.0 ** (-jnp.arange(0, head_dim, 2, dtype=jnp.float32) / head_dim)
    angles = jnp.arange(seq_len, dtype=jnp.float32)[:, None] * inv_freq[None, :]
    return jnp.cos(angles)[:, None, :], jnp.sin(angles)[:, None, :]


def rotate(values, cos_tab, sin_tab):
    half_dim = values.shape[-1] // 2
    x_first = values[..., :half_dim]
    x_second = values[..., half_dim:]
    return jnp.concatenate([x_first * cos_tab - x_second * sin_tab, x_second * cos_tab + x_first * sin_tab], axis=-1)


def gather_fsdp(weight, dim_index):
    return lax.all_gather(weight, 'fsdp', axis=dim_index, tiled=True)


def scatter_fsdp(grad_part, dim_index):
    return lax.psum_scatter(grad_part, 'fsdp', scatter_dimension=dim_index, tiled=True)


def device_step(x, grad_y, w_qkv, w_out, w_ff, w_down):
    seq_len = x.shape[1]
    head_dim = w_qkv.shape[3]
    score_scale = head_dim ** -0.5
    cos_tab, sin_tab = rope_tables(seq_len, head_dim)
    causal = jnp.arange(seq_len)[:, None] >= jnp.arange(seq_len)[None, :]

    x_f32 = x.astype(jnp.float32)
    normed1, inv_std1 = layer_norm(x_f32)
    normed1_b = normed1.astype(jnp.bfloat16)
    qkv_full = gather_fsdp(w_qkv, 0)
    qkv_raw = jnp.einsum('btd,dchn->btchn', normed1_b, qkv_full, preferred_element_type=jnp.float32)
    clip_keep = jnp.abs(qkv_raw) < 8.0
    qkv_cl = jnp.clip(qkv_raw, -8.0, 8.0)
    q_rot = rotate(qkv_cl[:, :, 0], cos_tab, sin_tab).astype(jnp.bfloat16)
    k_rot = rotate(qkv_cl[:, :, 1], cos_tab, sin_tab).astype(jnp.bfloat16)
    v_val = qkv_cl[:, :, 2].astype(jnp.bfloat16)
    scores = jnp.einsum('bqhe,bkhe->bhqk', q_rot, k_rot, preferred_element_type=jnp.float32) * score_scale
    prob_f32 = jax.nn.softmax(jnp.where(causal, scores, -1e30), axis=-1)
    prob_b16 = prob_f32.astype(jnp.bfloat16)
    attn_o = jnp.einsum('bhqk,bkhe->bqhe', prob_b16, v_val, preferred_element_type=jnp.float32).astype(jnp.bfloat16)
    out_full = gather_fsdp(w_out, 2)
    attn_part = jnp.einsum('crif,ife->cre', attn_o, out_full, preferred_element_type=jnp.float32)
    hidden = (x_f32 + lax.psum(attn_part, 'tp')).astype(jnp.bfloat16)
    hidden_f32 = hidden.astype(jnp.float32)
    normed2, inv_std2 = layer_norm(hidden_f32)
    normed2_b = normed2.astype(jnp.bfloat16)
    ff_full = gather_fsdp(w_ff, 0)
    up_gate = jnp.einsum('btd,dcf->btcf', normed2_b, ff_full, preferred_element_type=jnp.float32)
    up_val = up_gate[:, :, 0]
    gate_val = up_gate[:, :, 1]
    gate_sig = jax.nn.sigmoid(gate_val)
    gate_act = gate_val * gate_sig
    mlp_act = (gate_act * up_val).astype(jnp.bfloat16)
    down_full = gather_fsdp(w_down, 1)
    mlp_part = jnp.einsum('btf,fd->btd', mlp_act, down_full, preferred_element_type=jnp.float32)
    y_out = (hidden_f32 + lax.psum(mlp_part, 'tp')).astype(jnp.bfloat16)

    grad_y32 = grad_y.astype(jnp.float32)
    grad_down = scatter_fsdp(jnp.einsum('btf,btd->fd', mlp_act, grad_y, preferred_element_type=jnp.float32), 1)
    down_again = gather_fsdp(w_down, 1)
    grad_act = jnp.einsum('btd,fd->btf', grad_y, down_again, preferred_element_type=jnp.float32)
    grad_up = grad_act * gate_act
    grad_gate = grad_act * up_val * gate_sig * (1.0 + gate_val * (1.0 - gate_sig))
    grad_upgate = jnp.stack([grad_up, grad_gate], axis=2).astype(jnp.bfloat16)
    grad_ff = scatter_fsdp(jnp.einsum('btd,btcf->dcf', normed2_b, grad_upgate, preferred_element_type=jnp.float32), 0)
    ff_again = gather_fsdp(w_ff, 0)
    grad_norm2 = lax.psum(jnp.einsum('btcf,dcf->btd', grad_upgate, ff_again, preferred_element_type=jnp.float32), 'tp')
    grad_hidden = grad_y32 + norm_backward(grad_norm2, normed2, inv_std2)
    grad_hidden_b = grad_hidden.astype(jnp.bfloat16)
    grad_out = scatter_fsdp(jnp.einsum('crif,cre->ife', attn_o, grad_hidden_b, preferred_element_type=jnp.float32), 2)
    out_again = gather_fsdp(w_out, 2)
    grad_o = jnp.einsum('cre,ife->crif', grad_hidden_b, out_again, preferred_element_type=jnp.float32).astype(jnp.bfloat16)
    grad_prob = jnp.einsum('bqhe,bkhe->bhqk', grad_o, v_val, preferred_element_type=jnp.float32)
    grad_v = jnp.einsum('bhqk,bqhe->bkhe', prob_b16, grad_o, preferred_element_type=jnp.float32)
    grad_score = prob_f32 * (grad_prob - jnp.sum(grad_prob * prob_f32, axis=-1, keepdims=True))
    grad_score_b = (grad_score * score_scale).astype(jnp.bfloat16)
    grad_q = jnp.einsum('bhqk,bkhe->bqhe', grad_score_b, k_rot, preferred_element_type=jnp.float32)
    grad_k = jnp.einsum('bhqk,bqhe->bkhe', grad_score_b, q_rot, preferred_element_type=jnp.float32)
    grad_qkv_all = jnp.stack([rotate(grad_q, cos_tab, -sin_tab), rotate(grad_k, cos_tab, -sin_tab), grad_v], axis=2)
    grad_qkv_b = jnp.where(clip_keep, grad_qkv_all, 0.0).astype(jnp.bfloat16)
    grad_qkv = scatter_fsdp(jnp.einsum('btd,btchn->dchn', normed1_b, grad_qkv_b, preferred_element_type=jnp.float32), 0)
    qkv_again = gather_fsdp(w_qkv, 0)
    grad_norm1 = lax.psum(jnp.einsum('btchn,dchn->btd', grad_qkv_b, qkv_again, preferred_element_type=jnp.float32), 'tp')
    grad_x = (grad_hidden + norm_backward(grad_norm1, normed1, inv_std1)).astype(jnp.bfloat16)
    return y_out, grad_x, grad_qkv, grad_out, grad_ff, grad_down


def solution(mesh):
    act_spec = P('fsdp', None, None)
    weight_specs = (P('fsdp', None, 'tp', None), P('tp', None, 'fsdp'), P('fsdp', None, 'tp'), P('tp', 'fsdp'))
    return jax.shard_map(device_step, mesh=mesh, in_specs=(act_spec, act_spec) + weight_specs, out_specs=(act_spec, act_spec) + weight_specs, check_vma=False)
```

profile of v0, /device:TPU:0, one launch (start us, length us, event | category | flops | bytes accessed | tf_op | source)
XLA Modules:
  0.0 2175.9 jit_solution(1010923923019712257)
XLA Ops:
  19.1 64.7 %all-gather.5.cloned.1.call-done = bf16[2048,3,8,128]{0,3,2,1:T(8,128)(2,1)} async-done(((bf16[256,3,8,128]{0,3,2,1:T(8,128)(2,1)}), bf16[2048,3,8,128]{0,3,2,1:T(8,128)(2,1)}) %all-gather.5.cloned.1.call-update) | async-done | bytes 12582928 | tf_op jit(solution)/shard_map/all_gather | solution.py:34
  83.8 21.3 fusion.74
  105.1 11.9 copy_clamp_fusion
  124.0 11.6 fusion.127
  135.6 8.4 fusion.91
  144.0 9.8 convolution_bitcast_fusion.4
  153.9 7.1 copy.18
  161.7 186.3 %all-reduce.5.cloned.1.call-done = f32[2,512,2048]{2,1,0:T(8,128)} async-done(((f32[2,512,2048]{2,1,0:T(8,128)}), f32[2,512,2048]{2,1,0:T(8,128)}) %all-reduce.5.cloned.1.call-update) | async-done | bytes 8388624 | tf_op jit(solution)/shard_map/psum | solution.py:64
  356.8 150.8 %all-gather.9.cloned.1.call-done = bf16[2048,2,4096]{2,0,1:T(8,128)(2,1)} async-done(((bf16[256,2,4096]{2,0,1:T(8,128)(2,1)}), bf16[2048,2,4096]{2,0,1:T(8,128)(2,1)}) %all-gather.9.cloned.1.call-update) | async-done | bytes 33554448 | tf_op jit(solution)/shard_map/all_gather | solution.py:34
  507.7 42.1 %fusion.4 = f32[2,512,2,4096]{3,1,2,0:T(8,128)} fusion(bf16[2048,2,4096]{2,0,1:T(8,128)(2,1)} %all-gather.9.cloned.1.call-done, bf16[2,512,2048]{2,1,0:T(8,128)(2,1)} %copy-done.1, f32[2,512]{1,0:T(2,128)S(1)} %add_rsqrt_fusion, f32[2,512]{1,0:T(2,128)S(1)} %broadcast_multiply_fusion.4), kind=kOutput, calls=%fused_computation.4 | convolution fusion | flops 34368126976 | bytes 71311360 | tf_op jit(solution)/shard_map/btd,dcf->btcf/dot_general | solution.py:69
  549.8 48.8 %all-gather.11.cloned.1.call-done = bf16[4096,2048]{1,0:T(8,128)(2,1)} async-done(((bf16[4096,256]{1,0:T(8,128)(2,1)}), bf16[4096,2048]{1,0:T(8,128)(2,1)}) %all-gather.11.cloned.1.call-update) | async-done | bytes 16777232 | tf_op jit(solution)/shard_map/all_gather | solution.py:34
  598.6 33.8 %fusion.43 = (bf16[2,512,1,4096]{3,1,0,2:T(8,128)(2,1)}, bf16[2,512,1,4096]{3,1,0,2:T(8,128)(2,1)}, bf16[2,512,4096]{2,1,0:T(8,128)(2,1)}) fusion(f32[2,512,2,4096]{3,1,2,0:T(8,128)} %fusion.4, bf16[2,512,2048]{2,1,0:T(8,128)(2,1)} %param.7, bf16[4096,2048]{1,0:T(8,128)(2,1)} %all-gather.11.cloned.1.call-done), kind=kOutput, calls=%fused_computation.66 | convolution fusion | flops 17242783744 | bytes 79691776 | tf_op jit(solution)/shard_map/btd,fd->btf/dot_general | solution.py:82
  632.4 43.9 %fusion.57 = f32[2,512,2048]{2,1,0:T(8,128)} fusion(bf16[2048,2,4096]{2,0,1:T(8,128)(2,1)} %all-gather.9.cloned.1.call-done, bf16[2,512,1,4096]{3,1,0,2:T(8,128)(2,1)} %get-tuple-element.21, bf16[2,512,1,4096]{3,1,0,2:T(8,128)(2,1)} %get-tuple-element.20), kind=kOutput, calls=%fused_computation.77 | convolution fusion | flops 34368126976 | bytes 58720256 | tf_op jit(solution)/shard_map/btcf,dcf->btd/dot_general | solution.py:88
  676.4 24.2 %fusion.8 = f32[2,512,2048]{2,1,0:T(8,128)} fusion(bf16[2,512,4096]{2,1,0:T(8,128)(2,1)} %get-tuple-element.22, bf16[4096,2048]{1,0:T(8,128)(2,1)} %all-gather.11.cloned.1.call-done), kind=kOutput, calls=%fused_computation.13 | convolution fusion | flops 17179869184 | bytes 33554432 | tf_op jit(solution)/shard_map/btf,fd->btd/dot_general | solution.py:76
  700.5 169.9 %all-reduce.7.cloned.1.call-done = f32[2,512,2048]{2,1,0:T(8,128)} async-done(((f32[2,512,2048]{2,1,0:T(8,128)}), f32[2,512,2048]{2,1,0:T(8,128)}) %all-reduce.7.cloned.1.call-update) | async-done | bytes 8388624 | tf_op jit(solution)/shard_map/psum | solution.py:88
  893.0 10.0 fusion.77
  903.1 10.4 fusion.101
  913.5 25.3 %fusion.80 = f32[2,512,8,128]{1,3,2,0:T(8,128)} fusion(f32[2,8,512,512]{2,3,1,0:T(8,128)} %fusion.101, bf16[2,512,8,64]{1,3,2,0:T(8,128)(2,1)S(1)} %copy-done.14, bf16[2,512,8,64]{1,3,2,0:T(8,128)(2,1)} %get-tuple-element.36, f32[2,8,512,512]{2,3,1,0:T(8,128)} %get-tuple-element.41, f32[2,8,512]{2,1,0:T(8,128)S(1)} %copy-done.31), kind=kOutput, calls=%fused_computation.97 | convolution fusion | flops 1107304960 | bytes 39878656 | tf_op jit(solution)/shard_map/bhqk,bkhe->bqhe/dot_general | solution.py:98
  938.8 24.6 %fusion.83 = f32[2,512,8,128]{1,3,2,0:T(8,128)} fusion(f32[2,8,512,512]{2,3,1,0:T(8,128)} %fusion.101, bf16[2,512,8,64]{1,3,2,0:T(8,128)(2,1)S(1)} %copy-done.12, bf16[2,512,8,64]{1,3,2,0:T(8,128)(2,1)S(1)} %copy-done.10, f32[2,8,512,512]{2,3,1,0:T(8,128)} %get-tuple-element.41, f32[2,8,512]{2,1,0:T(8,128)S(1)} %copy-done.31), kind=kOutput, calls=%fused_computation.98 | convolution fusion | flops 1107304960 | bytes 39878656 | tf_op jit(solution)/shard_map/bhqk,bqhe->bkhe/dot_general | solution.py:99
  970.1 18.5 fusion.54
  989.2 20.8 convolution_bitcast_fusion.2
  1010.7 46.7 %convolution_bitcast_fusion = f32[2048,2,4096]{2,0,1:T(8,128)} fusion(bf16[2,512,1,4096]{3,1,0,2:T(8,128)(2,1)} %get-tuple-element.21, bf16[2,512,1,4096]{3,1,0,2:T(8,128)(2,1)} %get-tuple-element.20, bf16[2,512,2048]{2,1,0:T(8,128)(2,1)} %copy-done.1, f32[2,512]{1,0:T(2,128)S(1)} %copy-done.25, f32[2,512]{1,0:T(2,128)S(1)} %copy-done.20), kind=kOutput, calls=%fused_computation.6 | convolution fusion | flops 34401681408 | bytes 88088576 | tf_op jit(solution)/shard_map/btd,btcf->dcf/dot_general | solution.py:86
  1059.0 10.0 convolution_bitcast_fusion.3
  1069.1 25.9 %convolution_bitcast_fusion.1 = f32[4096,2048]{1,0:T(8,128)} fusion(bf16[2,512,4096]{2,1,0:T(8,128)(2,1)} %get-tuple-element.22, bf16[2,512,2048]{2,1,0:T(8,128)(2,1)} %param.7), kind=kOutput, calls=%fused_computation.7 | convolution fusion | flops 17179869184 | bytes 46137344 | tf_op jit(solution)/shard_map/btf,btd->fd/dot_general | solution.py:80
  1095.0 268.0 %all-reduce.9.cloned.1.call-done = (f32[2,512,2048]{2,1,0:T(8,128)}, f32[2,512,2048]{2,1,0:T(8,128)}) async-done(((f32[2,512,2048]{2,1,0:T(8,128)}, f32[2,512,2048]{2,1,0:T(8,128)}), (f32[2,512,2048]{2,1,0:T(8,128)}, f32[2,512,2048]{2,1,0:T(8,128)})) %all-reduce.9.cloned.1.call-update) | async-done | bytes 16777232 | tf_op jit(solution)/shard_map/psum | solution.py:77
  1368.9 7.1 fusion.42
  1376.0 8.6 fusion.39
  1384.6 131.6 %reduce-scatter.5.cloned.1.call-done = f32[256,3,8,128]{3,0,2,1:T(8,128)} async-done(((f32[2048,3,8,128]{3,0,2,1:T(8,128)}), f32[256,3,8,128]{3,0,2,1:T(8,128)}) %reduce-scatter.5.cloned.1.call-update) | async-done | bytes 3145744 | tf_op jit(solution)/shard_map/reduce_scatter | solution.py:38
  1521.6 375.6 %reduce-scatter.9.cloned.1.call-done = f32[256,2,4096]{2,0,1:T(8,128)} async-done(((f32[2048,2,4096]{2,0,1:T(8,128)}), f32[256,2,4096]{2,0,1:T(8,128)}) %reduce-scatter.9.cloned.1.call-update) | async-done | bytes 8388624 | tf_op jit(solution)/shard_map/reduce_scatter | solution.py:38
  1897.2 15.4 copy.36
  1912.6 53.5 %reduce-scatter.7.cloned.1.call-done = f32[8,128,256]{2,1,0:T(8,128)} async-done(((f32[8,128,2048]{2,1,0:T(8,128)}), f32[8,128,256]{2,1,0:T(8,128)}) %reduce-scatter.7.cloned.1.call-update) | async-done | bytes 1048592 | tf_op jit(solution)/shard_map/reduce_scatter | solution.py:38
  1966.1 203.1 %reduce-scatter.11.cloned.1.call-done = f32[4096,256]{1,0:T(8,128)} async-done(((f32[4096,2048]{1,0:T(8,128)}), f32[4096,256]{1,0:T(8,128)}) %reduce-scatter.11.cloned.1.call-update) | async-done | bytes 4194320 | tf_op jit(solution)/shard_map/reduce_scatter | solution.py:38
  (112 shorter events, 71.9 us)
Async XLA Ops:
  7.2 76.6 %all-gather.5.cloned.1.call-start = ((), (), s32[]{:S(2)}) async-start(), calls=%async_computation.4 | async-start | bytes 14155776 | tf_op jit(solution)/shard_map/all_gather | solution.py:34
  10.0 134.0 %all-gather.7.cloned.1.call-start = ((), (), s32[]{:S(2)}) async-start(), calls=%async_computation.5 | async-start | bytes 4718592 | tf_op jit(solution)/shard_map/all_gather | solution.py:34
  10.8 337.2 %all-reduce.5.cloned.1.call-start = ((), (), s32[]{:S(2)}) async-start(), calls=%async_computation.6 | async-start | bytes 16777216 | tf_op jit(solution)/shard_map/psum | solution.py:64
  14.5 90.6 %copy-start.16 = (f32[2,512]{1,0:T(2,128)}, f32[2,512]{1,0:T(2,128)S(1)}, u32[]{:S(2)}) copy-start(f32[2,512]{1,0:T(2,128)S(1)} %broadcast_multiply_fusion.5) | copy-start | bytes 12292
  17.9 87.2 %copy-start.21 = (f32[2,512]{1,0:T(2,128)}, f32[2,512]{1,0:T(2,128)S(1)}, u32[]{:S(2)}) copy-start(f32[2,512]{1,0:T(2,128)S(1)} %add_rsqrt_fusion.1) | copy-start | bytes 12292
  19.1 102.3 %copy-start.7 = (f32[512,64]{0,1:T(8,128)}, f32[512,64]{0,1:T(8,128)S(1)}, u32[]{:S(2)}) copy-start(f32[512,64]{0,1:T(8,128)S(1)} %get-tuple-element.39) | copy-start | bytes 393220
  124.0 11.6 copy-start.9
  124.0 11.6 copy-start.11
  124.0 11.6 copy-start.13
  135.6 8.4 copy-start.30
  144.0 9.8 copy-start.26
  153.8 353.8 %all-gather.9.cloned.1.call-start = ((), (), s32[]{:S(2)}) async-start(), calls=%async_computation.7 | async-start | bytes 37748736 | tf_op jit(solution)/shard_map/all_gather | solution.py:34
  161.0 437.6 %all-gather.11.cloned.1.call-start = ((), (), s32[]{:S(2)}) async-start(), calls=%async_computation.8 | async-start | bytes 18874368 | tf_op jit(solution)/shard_map/all_gather | solution.py:34
  161.6 708.8 %all-reduce.7.cloned.1.call-start = ((), (), s32[]{:S(2)}) async-start(), calls=%async_computation.9 | async-start | bytes 16777216 | tf_op jit(solution)/shard_map/psum | solution.py:88
  353.6 196.2 %copy-start.18 = (f32[2,512]{1,0:T(2,128)}, f32[2,512]{1,0:T(2,128)S(1)}, u32[]{:S(2)}) copy-start(f32[2,512]{1,0:T(2,128)S(1)} %broadcast_multiply_fusion.4) | copy-start | bytes 12292
  356.8 193.0 %copy-start.23 = (f32[2,512]{1,0:T(2,128)}, f32[2,512]{1,0:T(2,128)S(1)}, u32[]{:S(2)}) copy-start(f32[2,512]{1,0:T(2,128)S(1)} %add_rsqrt_fusion) | copy-start | bytes 12292
  676.3 686.8 %all-reduce.9.cloned.1.call-start = ((), (), s32[]{:S(2)}) async-start(), calls=%async_computation.14 | async-start | bytes 33554432 | tf_op jit(solution)/shard_map/psum | solution.py:77
  676.3 194.1 %copy-start.19 = (f32[2,512]{1,0:T(2,128)S(1)}, f32[2,512]{1,0:T(2,128)}, u32[]{:S(2)}) copy-start(f32[2,512]{1,0:T(2,128)} %copy-done.18) | copy-start | bytes 12292
  676.4 194.1 %copy-start.24 = (f32[2,512]{1,0:T(2,128)S(1)}, f32[2,512]{1,0:T(2,128)}, u32[]{:S(2)}) copy-start(f32[2,512]{1,0:T(2,128)} %copy-done.23) | copy-start | bytes 12292
  870.5 8.3 copy-start.4
  903.1 10.4 copy-start.14
  913.5 25.3 %copy-start.10 = (bf16[2,512,8,64]{1,3,2,0:T(8,128)(2,1)S(1)}, bf16[2,512,8,64]{1,3,2,0:T(8,128)(2,1)}, u32[]{:S(2)}) copy-start(bf16[2,512,8,64]{1,3,2,0:T(8,128)(2,1)} %copy-done.9) | copy-start | bytes 3145732
  913.5 25.3 %copy-start.12 = (bf16[2,512,8,64]{1,3,2,0:T(8,128)(2,1)S(1)}, bf16[2,512,8,64]{1,3,2,0:T(8,128)(2,1)}, u32[]{:S(2)}) copy-start(bf16[2,512,8,64]{1,3,2,0:T(8,128)(2,1)} %copy-done.11) | copy-start | bytes 3145732
  938.7 24.6 %copy-start.8 = (f32[512,64]{0,1:T(8,128)S(1)}, f32[512,64]{0,1:T(8,128)}, u32[]{:S(2)}) copy-start(f32[512,64]{0,1:T(8,128)} %copy-done.7) | copy-start | bytes 393220
  938.8 24.6 %copy-start.15 = (f32[512,64]{0,1:T(8,128)S(1)}, f32[512,64]{0,1:T(8,128)}, u32[]{:S(2)}) copy-start(f32[512,64]{0,1:T(8,128)} %get-tuple-element.37) | copy-start | bytes 393220
  963.4 6.7 copy-start.28
  963.4 6.7 copy-start.29
  988.6 527.6 %reduce-scatter.5.cloned.1.call-start = ((), (), s32[]{:S(2)}) async-start(), calls=%async_computation.10 | async-start | bytes 28311552 | tf_op jit(solution)/shard_map/reduce_scatter | solution.py:38
  1010.1 887.2 %reduce-scatter.9.cloned.1.call-start = ((), (), s32[]{:S(2)}) async-start(), calls=%async_computation.12 | async-start | bytes 75497472 | tf_op jit(solution)/shard_map/reduce_scatter | solution.py:38
  1057.5 908.6 %reduce-scatter.7.cloned.1.call-start = ((), (), s32[]{:S(2)}) async-start(), calls=%async_computation.11 | async-start | bytes 9437184 | tf_op jit(solution)/shard_map/reduce_scatter | solution.py:38
  1069.1 1100.1 %reduce-scatter.11.cloned.1.call-start = ((), (), s32[]{:S(2)}) async-start(), calls=%async_computation.13 | async-start | bytes 37748736 | tf_op jit(solution)/shard_map/reduce_scatter | solution.py:38
  1368.9 7.1 copy-start
  (11 other events, 29.0 us)
Sparse Core Ops, SparseCore 0:
  10.4 73.3 all-gather.4
  85.7 33.3 all-gather.6
  153.9 193.9 all-reduce.4
  350.3 157.3 all-gather.8
  509.4 89.1 all-gather.10
  676.4 193.9 all-reduce.6
  988.7 374.3 all-reduce.8
  1366.6 149.5 reduce-scatter.4
  1519.8 377.4 reduce-scatter.8
  1901.1 64.9 reduce-scatter.6
  1970.2 198.9 reduce-scatter.10
where the time goes:
time: 2180 us
  waiting for transfers between devices  1650 us (76%)
  matrix products  394 us (18%)
  other arithmetic  66.7 us (3%)
  local copies, waits for them, and re-layouts  47 us (2%)
    reduce_scatter x4, waiting for transfers between devices, scatter_fsdp(): lax.psum_scatter(grad_part, 'fsdp', scatter_dimension=dim_index, tiled=True)  764 us
    psum x1, waiting for transfers between devices, device_step(): y_out = (hidden_f32 + lax.psum(mlp_part, 'tp')).astype(jnp.bfloat16)  268 us
    all_gather x4, waiting for transfers between devices, gather_fsdp(): return lax.all_gather(weight, 'fsdp', axis=dim_index, tiled=True)  264 us
    psum x1, waiting for transfers between devices, device_step(): hidden = (x_f32 + lax.psum(attn_part, 'tp')).astype(jnp.bfloat16)  186 us
    psum x1, waiting for transfers between devices, device_step(): lax.psum(jnp.einsum('btcf,dcf->btd', grad_upgate, ff_again, preferred_ele...  170 us
    dot_general x1, matrix products, device_step(): jnp.einsum('btd,btcf->dcf', normed2_b, grad_upgate, preferred_element_typ...  46.7 us
    dot_general x1, matrix products, device_step(): jnp.einsum('btcf,dcf->btd', grad_upgate, ff_again, preferred_element_type...  43.9 us
  transfers between devices with their start and end apart: 11, of which 10 were waited for; matrix products, arithmetic and copies ran while one was open for 14% of the time, Pallas kernels for 0%

commit v1 on v0

v1 whole, which is shorter than its diff:
```python
import functools

import jax
import jax.numpy as jnp
import numpy as np
from jax import lax
from jax.experimental import pallas as pl
from jax.experimental.pallas import tpu as pltpu
from jax.sharding import Mesh, PartitionSpec as P


F32 = jnp.float32
BF16 = jnp.bfloat16
SWAP = [(0, 1), (1, 0)]
EPS = 1e-5
CLIP = 8.0
SHARD = 256
VMEM_LIMIT = 60 * 1024 * 1024


def dot_nn(a, b):
    return lax.dot_general(a, b, (((1,), (0,)), ((), ())), preferred_element_type=F32)


def dot_nt(a, b):
    return lax.dot_general(a, b, (((1,), (1,)), ((), ())), preferred_element_type=F32)


def dot_tn(a, b):
    return lax.dot_general(a, b, (((0,), (0,)), ((), ())), preferred_element_type=F32)


def norm_stats(values):
    mean_val = jnp.mean(values, axis=-1, keepdims=True)
    centered = values - mean_val
    inv_std = lax.rsqrt(jnp.mean(centered * centered, axis=-1, keepdims=True) + EPS)
    return centered * inv_std, inv_std


def norm_backward(grad_norm, normed, inv_std):
    grad_mean = jnp.mean(grad_norm, axis=-1, keepdims=True)
    proj_mean = jnp.mean(grad_norm * normed, axis=-1, keepdims=True)
    return inv_std * (grad_norm - grad_mean - normed * proj_mean)


def call(kernel, grid, in_specs, out_specs, out_shape, ids, operands, flops, scratch=(), aliases=None):
    nbytes = sum(int(np.prod(o.shape)) * o.dtype.itemsize for o in operands)
    nbytes += sum(int(np.prod(o.shape)) * o.dtype.itemsize for o in jax.tree.leaves(out_shape))
    return pl.pallas_call(
        kernel,
        out_shape=out_shape,
        grid_spec=pltpu.PrefetchScalarGridSpec(
            num_scalar_prefetch=1, grid=grid, in_specs=in_specs, out_specs=out_specs, scratch_shapes=scratch
        ),
        input_output_aliases=aliases or {},
        compiler_params=pltpu.CompilerParams(
            dimension_semantics=('arbitrary',) * len(grid), vmem_limit_bytes=VMEM_LIMIT
        ),
        cost_estimate=pl.CostEstimate(flops=int(flops), bytes_accessed=int(nbytes), transcendentals=0),
    )(ids, *operands)


def sds(shape, dtype):
    return jax.ShapeDtypeStruct(shape, dtype)


def column_order(block, width):
    n = width // SHARD
    return [block[:, s * SHARD:(s + 1) * SHARD] for s in list(range(0, n, 2)) + list(range(1, n, 2))]


def ln1_kernel(ids, x_ref, gy_ref, n1_ref, xp_ref, gyp_ref):
    width = x_ref.shape[1]
    x = jnp.concatenate(column_order(x_ref, width), axis=1)
    xp_ref[...] = x
    gyp_ref[...] = jnp.concatenate(column_order(gy_ref, width), axis=1)
    normed, _ = norm_stats(x.astype(F32))
    n1_ref[...] = normed.astype(BF16)


def qkv_kernel(ids, n1_ref, w_ref, cos_ref, sin_ref, out_ref, keep_ref, *, rotated):
    raw = dot_nn(n1_ref[...], w_ref[...])
    keep_ref[...] = (jnp.abs(raw) < CLIP).astype(BF16)
    clipped = jnp.clip(raw, -CLIP, CLIP)
    seq, head = cos_ref.shape
    rows, cols = clipped.shape

    @pl.when(pl.program_id(0) < rotated)
    def _():
        for r in range(rows // seq):
            for c in range(cols // head):
                part = clipped[r * seq:(r + 1) * seq, c * head:(c + 1) * head]
                turned = part * cos_ref[...] + pltpu.roll(part, head // 2, 1) * sin_ref[...]
                out_ref[r * seq:(r + 1) * seq, c * head:(c + 1) * head] = turned.astype(BF16)

    @pl.when(pl.program_id(0) >= rotated)
    def _():
        out_ref[...] = clipped.astype(BF16)


def softmax_rows(q, k, first_row, scale):
    s = dot_nt(q, k) * scale
    row = first_row + lax.broadcasted_iota(jnp.int32, s.shape, 0)
    col = lax.broadcasted_iota(jnp.int32, s.shape, 1)
    s = jnp.where(row >= col, s, -1e30)
    e = jnp.exp(s - jnp.max(s, axis=-1, keepdims=True))
    return e / jnp.sum(e, axis=-1, keepdims=True)


def attn_kernel(ids, q_ref, k_ref, v_ref, o_ref, *, head, scale, rows):
    seq, cols = q_ref.shape
    for c in range(cols // head):
        cs = slice(c * head, (c + 1) * head)
        for r in range(seq // rows):
            rs = slice(r * rows, (r + 1) * rows)
            ks = slice(0, (r + 1) * rows)
            p = softmax_rows(q_ref[rs, cs], k_ref[ks, cs], r * rows, scale).astype(BF16)
            o_ref[rs, cs] = dot_nn(p, v_ref[ks, cs]).astype(BF16)


def attn_bwd_kernel(ids, q_ref, k_ref, v_ref, do_ref, keep_ref, cos_ref, sin_ref, out_ref, dk_acc, dv_acc, *, head, scale, rows):
    seq, cols = q_ref.shape
    for c in range(cols // head):
        cs = slice(c * head, (c + 1) * head)
        for r in reversed(range(seq // rows)):
            rs = slice(r * rows, (r + 1) * rows)
            ks = slice(0, (r + 1) * rows)
            q, k, v, do = q_ref[rs, cs], k_ref[ks, cs], v_ref[ks, cs], do_ref[rs, cs]
            p = softmax_rows(q, k, r * rows, scale)
            dp = dot_nt(do, v)
            ds = (p * (dp - jnp.sum(dp * p, axis=-1, keepdims=True)) * scale).astype(BF16)
            dv = dot_tn(p.astype(BF16), do)
            dk = dot_tn(ds, q)
            dq = dot_nn(ds, k)
            dq = dq * cos_ref[rs] - pltpu.roll(dq, head // 2, 1) * sin_ref[rs]
            out_ref[0, rs, cs] = jnp.where(keep_ref[0, rs, cs] > 0, dq, 0.0).astype(BF16)
            if r == seq // rows - 1:
                dk_acc[...] = dk
                dv_acc[...] = dv
            else:
                dk_acc[ks] += dk
                dv_acc[ks] += dv
        dk = dk_acc[...]
        dk = dk * cos_ref[...] - pltpu.roll(dk, head // 2, 1) * sin_ref[...]
        out_ref[1, :, cs] = jnp.where(keep_ref[1, :, cs] > 0, dk, 0.0).astype(BF16)
        out_ref[2, :, cs] = jnp.where(keep_ref[2, :, cs] > 0, dv_acc[...], 0.0).astype(BF16)


def nn_kernel(ids, *refs):
    *a_refs, w_ref, out_ref = refs
    depth = w_ref.shape[0] // len(a_refs)
    total = dot_nn(a_refs[0][...], w_ref[0:depth])
    for i, a_ref in enumerate(a_refs[1:], 1):
        total += dot_nn(a_ref[...], w_ref[i * depth:(i + 1) * depth])
    out_ref[...] = total


def combine1_kernel(ids, x_ref, part_ref, recv_ref, h_ref, n2_ref):
    h = (x_ref[...].astype(F32) + (part_ref[...] + recv_ref[...])).astype(BF16)
    h_ref[...] = h
    normed, _ = norm_stats(h.astype(F32))
    n2_ref[...] = normed.astype(BF16)


def ffn_kernel(ids, theirs_ref, mine_ref, wu_ref, wg_ref, u_ref, g_ref, act_ref, n2_ref):
    half = theirs_ref.shape[0]

    @pl.when(pl.program_id(0) == 0)
    def _():
        n2_ref[0:half] = theirs_ref[...]
        n2_ref[half:] = mine_ref[...]

    u = dot_nn(n2_ref[...], wu_ref[0])
    g = dot_nn(n2_ref[...], wg_ref[0])
    u_ref[...] = u
    g_ref[...] = g
    act_ref[...] = (g * jax.nn.sigmoid(g) * u).astype(BF16)


def dswiglu_kernel(ids, gy_ref, w_ref, u_ref, g_ref, out_ref):
    grad_act = dot_nt(gy_ref[...], w_ref[...])
    u, g = u_ref[...], g_ref[...]
    sig = jax.nn.sigmoid(g)
    out_ref[0] = (grad_act * (g * sig)).astype(BF16)
    out_ref[1] = (grad_act * u * sig * (1.0 + g * (1.0 - sig))).astype(BF16)


def grad_n2_kernel(ids, lo_ref, hi_ref, w_ref, out_ref):
    depth = lo_ref.shape[2]
    total = dot_nt(lo_ref[0], w_ref[0, :, 0:depth])
    total += dot_nt(hi_ref[0], w_ref[0, :, depth:])
    total += dot_nt(lo_ref[1], w_ref[1, :, 0:depth])
    total += dot_nt(hi_ref[1], w_ref[1, :, depth:])
    out_ref[...] = total


def combine2_kernel(ids, gy_ref, h_ref, part_ref, recv_ref, gh_ref, ghb_ref):
    normed, inv_std = norm_stats(h_ref[...].astype(F32))
    gh = gy_ref[...].astype(F32) + norm_backward(part_ref[...] + recv_ref[...], normed, inv_std)
    gh_ref[...] = gh
    ghb_ref[...] = gh.astype(BF16)


def grad_o_kernel(ids, theirs_ref, mine_ref, w_ref, out_ref, gh_ref):
    half = theirs_ref.shape[0]

    @pl.when(pl.program_id(0) == 0)
    def _():
        gh_ref[0:half] = theirs_ref[...]
        gh_ref[half:] = mine_ref[...]

    out_ref[...] = dot_nt(gh_ref[...], w_ref[...]).astype(BF16)


def grad_n1_kernel(ids, d_ref, w_ref, out_ref):
    depth = d_ref.shape[2]
    total = dot_nt(d_ref[0], w_ref[:, 0:depth])
    total += dot_nt(d_ref[1], w_ref[:, depth:2 * depth])
    total += dot_nt(d_ref[2], w_ref[:, 2 * depth:])
    out_ref[...] = total


def wgrad_rows_kernel(ids, a_ref, a2_ref, b_ref, b2_ref, *rest):
    *_, out_ref, at_ref = rest
    tokens = a_ref.shape[0]

    @pl.when((pl.program_id(0) == 0) & (pl.program_id(1) == 0))
    def _():
        at_ref[:, 0:tokens] = a_ref[...].T
        at_ref[:, tokens:] = a2_ref[...].T

    total = dot_nn(at_ref[:, 0:tokens], b_ref[0]) + dot_nn(at_ref[:, tokens:], b2_ref[0])
    out_ref[...] = total.reshape(out_ref.shape)


def wgrad_cols_kernel(ids, a_ref, a2_ref, b_ref, b2_ref, *rest):
    out_ref = rest[-1]
    total = dot_tn(a_ref[...], b_ref[...]) + dot_tn(a2_ref[...], b2_ref[...])
    for i in range(out_ref.shape[0]):
        out_ref[i] = total[:, i * SHARD:(i + 1) * SHARD]


def natural_order(values):
    n = values.shape[1] // SHARD
    blocks = [values[:, s * SHARD:(s + 1) * SHARD] for s in range(n)]
    return jnp.concatenate([blocks[(b % 2) * (n // 2) + b // 2] for b in range(n)], axis=1)


def y_kernel(ids, h_ref, part_ref, recv_ref, y_ref):
    y = (h_ref[...].astype(F32) + (part_ref[...] + recv_ref[...])).astype(BF16)
    y_ref[...] = natural_order(y)


def gx_kernel(ids, gh_ref, x_ref, part_ref, recv_ref, gx_ref):
    normed, inv_std = norm_stats(x_ref[...].astype(F32))
    gx = gh_ref[...] + norm_backward(part_ref[...] + recv_ref[...], normed, inv_std)
    gx_ref[...] = natural_order(gx.astype(BF16))


def other_z(value):
    return lax.ppermute(value, 'z', SWAP)


def other_core(value):
    return lax.ppermute(value, 'c', SWAP)


def after(value, *others):
    return lax.optimization_barrier((value,) + others)[0]


def gather(weight, axis):
    return lax.all_gather(weight, ('c', 'y', 'x'), axis=axis, tiled=True)


def scatter(grad, axis):
    return lax.psum_scatter(grad, ('y', 'x'), scatter_dimension=axis, tiled=True)


def layer(x, grad_y, w_qkv, w_out, w_ff, w_down):
    batch, seq, width = x.shape
    heads, head = w_qkv.shape[2:]
    inner = heads * head
    units = w_ff.shape[2]
    tokens = batch * seq
    half = tokens // 2
    chips = width // (2 * SHARD)
    z = lax.axis_index('z')
    core = lax.axis_index('c')
    ids = jnp.stack([z, core]).astype(jnp.int32)
    scale = head ** -0.5

    inv_freq = 10000.0 ** (-jnp.arange(0, head, 2, dtype=F32) / head)
    angles = jnp.arange(seq, dtype=F32)[:, None] * inv_freq[None, :]
    cos_tab = jnp.concatenate([jnp.cos(angles), jnp.cos(angles)], axis=1)
    sin_tab = jnp.concatenate([-jnp.sin(angles), jnp.sin(angles)], axis=1)

    qkv_full = gather(w_qkv.reshape(w_qkv.shape[0], 3 * inner), 0)
    out_full = gather(w_out.reshape(inner, w_out.shape[2]), 1)
    ff_full = gather(jnp.transpose(w_ff, (1, 0, 2)), 1)
    down_full = gather(w_down, 1)

    br = 128
    per_half = half // br
    src = lambda i, s: (((i // per_half + s[0] + 1) % 2) * per_half + i % per_half, 0)
    row = lambda i, s: (i, 0)
    n1, xp, gyp = call(
        ln1_kernel, (tokens // br,),
        [pl.BlockSpec((br, width), src)] * 2, [pl.BlockSpec((br, width), row)] * 3,
        [sds((tokens, width), BF16)] * 3, ids,
        [x.reshape(tokens, width), grad_y.reshape(tokens, width)], 20 * tokens * width)

    bn = 512
    fixed = lambda *_: (0, 0)
    n_qkv = 3 * inner // bn
    qkv, keep = call(
        functools.partial(qkv_kernel, rotated=2 * inner // bn), (n_qkv,),
        [pl.BlockSpec((tokens, width), fixed), pl.BlockSpec((width, bn), lambda j, s: (0, j)),
         pl.BlockSpec((seq, head), fixed), pl.BlockSpec((seq, head), fixed)],
        [pl.BlockSpec((tokens, bn), lambda j, s: (0, j)), pl.BlockSpec((None, tokens, bn), lambda j, s: (j // (n_qkv // 3), 0, j % (n_qkv // 3)))],
        [sds((tokens, 3 * inner), BF16), sds((3, tokens, inner), BF16)], ids,
        [n1, qkv_full, cos_tab, sin_tab], 2 * tokens * width * 3 * inner)

    bh = 256
    n_h = inner // bh
    qkv_spec = [pl.BlockSpec((seq, bh), lambda b, h, s, p=p: (b, p * n_h + h)) for p in range(3)]
    attn_o = call(
        functools.partial(attn_kernel, head=head, scale=scale, rows=256), (batch, n_h),
        qkv_spec, pl.BlockSpec((seq, bh), lambda b, h, s: (b, h)), sds((tokens, inner), BF16), ids,
        [qkv, qkv, qkv], 4 * tokens * seq * inner)

    def nn(lhs, w, r):
        depth = lhs[0].shape[1]
        return call(
            nn_kernel, (width // bn,),
            [pl.BlockSpec((half, depth), lambda j, s: (r, 0))] * len(lhs) + [pl.BlockSpec((depth * len(lhs), bn), lambda j, s: (0, j))],
            pl.BlockSpec((half, bn), lambda j, s: (0, j)), sds((half, width), F32), ids,
            [*lhs, w], 2 * half * depth * len(lhs) * width)

    part_theirs = nn([attn_o], out_full, 0)
    part_mine = nn([after(attn_o, part_theirs)], out_full, 1)
    mine_rows = lambda i, s: (per_half + i, 0)
    block = pl.BlockSpec((br, width), row)
    hidden, n2_mine = call(
        combine1_kernel, (per_half,), [pl.BlockSpec((br, width), mine_rows), block, block], [block, block],
        [sds((half, width), BF16)] * 2, ids, [xp, part_mine, other_z(part_theirs)], 20 * half * width)
    n2_theirs = other_z(n2_mine)

    bf = 256
    hu = units // 2

    def ffn(k, dep):
        nb = hu // bf
        up, gate, act, n2 = call(
            ffn_kernel, (nb,),
            [pl.BlockSpec((half, width), fixed)] * 2
            + [pl.BlockSpec((1, width, bf), lambda j, s, c=c: (c, 0, k * nb + j)) for c in range(2)],
            [pl.BlockSpec((tokens, bf), lambda j, s: (0, j))] * 3 + [pl.BlockSpec((tokens, width), fixed)],
            [sds((tokens, hu), F32)] * 2 + [sds((tokens, hu), BF16), sds((tokens, width), BF16)], ids,
            [after(n2_theirs, *dep), n2_mine, ff_full, ff_full], 4 * tokens * width * hu)
        return up, gate, act, n2

    up0, gate0, act0, n2 = ffn(0, ())
    up1, gate1, act1, _ = ffn(1, (act0,))
    act_sib = (other_core(act0), other_core(act1))
    gyp_sib = other_core(gyp)
    n2_sib = other_core(n2)
    n1_sib = other_core(n1)
    o_sib = other_core(attn_o)

    ba = 512
    mine_half = lambda *a: (0, a[-1][1])

    def wgrad_cols(a, a2, b, b2, total_rows, first, buf, dep):
        n = a.shape[1] // ba
        extra = [] if buf is None else [buf]
        return call(
            wgrad_cols_kernel, (n,),
            [pl.BlockSpec((tokens, ba), lambda j, s: (0, j))] * 2 + [pl.BlockSpec((tokens, width // 2), mine_half)] * 2
            + [pl.BlockSpec(memory_space=pl.ANY)] * len(extra),
            pl.BlockSpec((chips, ba, SHARD), lambda j, s: (0, first + j, 0)), sds((chips, total_rows, SHARD), F32), ids,
            [after(a, *dep), a2, b, b2, *extra], 4 * tokens * a.shape[1] * width // 2, aliases={5: 0} if extra else None)

    gd = wgrad_cols(act0, act_sib[0], gyp, gyp_sib, units, 0, None, (act1,))
    gd = wgrad_cols(act1, act_sib[1], gyp, gyp_sib, units, hu // ba, gd, ())
    grad_down = scatter(gd.reshape(chips * units, SHARD), 0)

    def dswiglu(k, up, gate, dep):
        nb = hu // bf
        return call(
            dswiglu_kernel, (nb,),
            [pl.BlockSpec((tokens, width), fixed), pl.BlockSpec((bf, width), lambda j, s: (k * nb + j, 0))]
            + [pl.BlockSpec((tokens, bf), lambda j, s: (0, j))] * 2,
            pl.BlockSpec((2, tokens, bf), lambda j, s: (0, 0, j)), sds((2, tokens, hu), BF16), ids,
            [after(gyp, *dep), down_full, up, gate], 2 * tokens * width * hu)

    d0 = dswiglu(0, up0, gate0, (gd,))
    d1 = dswiglu(1, up1, gate1, (d0,))
    d0_sib = other_core(d0)
    d1_sib = other_core(d1)

    def grad_n2(r, dep):
        bd = 256
        return call(
            grad_n2_kernel, (width // bd,),
            [pl.BlockSpec((2, half, hu), lambda j, s: (0, r, 0))] * 2 + [pl.BlockSpec((2, bd, units), lambda j, s: (0, j, 0))],
            pl.BlockSpec((half, bd), lambda j, s: (0, j)), sds((half, width), F32), ids,
            [after(d0, *dep), d1, ff_full], 4 * half * width * units)

    gn2_theirs = grad_n2(0, ())
    gn2_mine = grad_n2(1, (gn2_theirs,))

    def wgrad_ff(k, b, b2, buf, dep):
        n = hu // bn
        extra = [] if buf is None else [buf]
        return call(
            wgrad_rows_kernel, (2, n),
            [pl.BlockSpec((tokens, width // 2), mine_half)] * 2 + [pl.BlockSpec((1, tokens, bn), lambda c, j, s: (c, 0, j))] * 2
            + [pl.BlockSpec(memory_space=pl.ANY)] * len(extra),
            pl.BlockSpec((1, width // 2, bn), lambda c, j, s: (c, 0, k * n + j)), sds((2, width // 2, units), F32), ids,
            [after(n2, *dep), n2_sib, b, b2, *extra], 8 * tokens * width // 2 * hu,
            scratch=[pltpu.VMEM((width // 2, 2 * tokens), BF16)], aliases={5: 0} if extra else None)

    gff = wgrad_ff(0, d0, d0_sib, None, (gn2_mine,))
    gff = wgrad_ff(1, d1, d1_sib, gff, ())
    grad_ff = jnp.transpose(scatter(gff, 1), (1, 0, 2))

    gh, gh_mine = call(
        combine2_kernel, (per_half,),
        [pl.BlockSpec((br, width), mine_rows), block, block, block], [block, block],
        [sds((half, width), F32), sds((half, width), BF16)], ids,
        [after(gyp, gff), hidden, gn2_mine, other_z(gn2_theirs)], 20 * half * width)

    y_theirs = nn([after(act0, gh_mine), act1], down_full, 0)
    y_mine = nn([after(act0, y_theirs), act1], down_full, 1)

    grad_o, ghb = call(
        grad_o_kernel, (inner // bn,),
        [pl.BlockSpec((half, width), fixed)] * 2 + [pl.BlockSpec((bn, width), lambda j, s: (j, 0))],
        [pl.BlockSpec((tokens, bn), lambda j, s: (0, j)), pl.BlockSpec((tokens, width), fixed)],
        [sds((tokens, inner), BF16), sds((tokens, width), BF16)], ids,
        [other_z(gh_mine), after(gh_mine, y_mine), out_full], 2 * tokens * width * inner)
    gh_sib = other_core(ghb)
    dqkv = call(
        functools.partial(attn_bwd_kernel, head=head, scale=scale, rows=256), (batch, n_h),
        qkv_spec + [pl.BlockSpec((seq, bh), lambda b, h, s: (b, h)), pl.BlockSpec((3, seq, bh), lambda b, h, s: (0, b, h)),
                    pl.BlockSpec((seq, head), fixed), pl.BlockSpec((seq, head), fixed)],
        pl.BlockSpec((3, seq, bh), lambda b, h, s: (0, b, h)), sds((3, tokens, inner), BF16), ids,
        [qkv, qkv, qkv, grad_o, keep, cos_tab, sin_tab], 10 * tokens * seq * inner,
        scratch=[pltpu.VMEM((seq, head), F32)] * 2)
    dqkv_sib = other_core(dqkv)

    def grad_n1(r, dep):
        return call(
            grad_n1_kernel, (width // bn,),
            [pl.BlockSpec((3, half, inner), lambda j, s: (0, r, 0)), pl.BlockSpec((bn, 3 * inner), lambda j, s: (j, 0))],
            pl.BlockSpec((half, bn), lambda j, s: (0, j)), sds((half, width), F32), ids,
            [after(dqkv, *dep), qkv_full], 2 * half * width * 3 * inner)

    gn1_theirs = grad_n1(0, ())
    gn1_mine = grad_n1(1, (gn1_theirs,))
    go = wgrad_cols(attn_o, o_sib, ghb, gh_sib, inner, 0, None, (gn1_mine,))
    grad_out = scatter(go.reshape(chips * inner, SHARD), 0).reshape(heads, head, SHARD)
    gq = call(
        wgrad_rows_kernel, (3, inner // bn),
        [pl.BlockSpec((tokens, width // 2), mine_half)] * 2 + [pl.BlockSpec((1, tokens, bn), lambda c, j, s: (c, 0, j))] * 2,
        pl.BlockSpec((width // 2, bn), lambda c, j, s: (0, c * (inner // bn) + j)), sds((width // 2, 3 * inner), F32), ids,
        [after(n1, go), n1_sib, dqkv, dqkv_sib], 4 * tokens * width // 2 * 3 * inner,
        scratch=[pltpu.VMEM((width // 2, 2 * tokens), BF16)])
    grad_qkv = scatter(gq, 0).reshape(SHARD, 3, heads, head)

    def in_order(theirs, mine):
        both = jnp.where(z == 0, jnp.concatenate([mine, theirs], 0), jnp.concatenate([theirs, mine], 0))
        return both.reshape(batch, seq, width)

    y_own = call(
        y_kernel, (per_half,), [block] * 3, block, sds((half, width), BF16), ids,
        [after(hidden, gq), y_mine, other_z(y_theirs)], 4 * half * width)
    y_out = in_order(other_z(y_own), y_own)
    gx_own = call(
        gx_kernel, (per_half,), [block, pl.BlockSpec((br, width), mine_rows), block, block], block,
        sds((half, width), BF16), ids, [after(gh, y_own), xp, gn1_mine, other_z(gn1_theirs)], 20 * half * width)
    grad_x = in_order(other_z(gx_own), gx_own)
    return y_out, grad_x, grad_qkv, grad_out, grad_ff, grad_down


def solution(mesh):
    fine = Mesh(np.asarray(mesh.devices).reshape(2, 2, 2, 2), ('z', 'y', 'x', 'c'))
    fsdp = ('y', 'x', 'c')
    act_spec = P(fsdp, None, None)
    weight_specs = (P(fsdp, None, 'z', None), P('z', None, fsdp), P(fsdp, None, 'z'), P('z', fsdp))
    return jax.shard_map(layer, mesh=fine, in_specs=(act_spec, act_spec) + weight_specs, out_specs=(act_spec, act_spec) + weight_specs, check_vma=False)
```

time: 2180 us -> 1300 us (0.60)
  waiting for transfers between devices: 1650 us -> 781 us
  Pallas kernels: 0 us -> 439 us
  matrix products: 394 us -> 0 us
  other arithmetic: 66.7 us -> 12.9 us
    psum x3 -> x0, waiting for transfers between devices: 624 us -> none  [the longest x1 268 us: device_step(): y_out = (hidden_f32 + lax.psum(mlp_part, 'tp')).astype(jnp.bfloat16)]
    reduce_scatter x4, waiting for transfers between devices: 764 us -> 311 us  [scatter(): lax.psum_scatter(grad, ('y', 'x'), scatter_dimension=axis, tiled=True)]
    pallas_call x0 -> x27, Pallas kernels: none -> 439 us  [call(): pl.pallas_call(kernel, out_shape=out_shape, grid_spec=pltpu.PrefetchScala...]
    ppermute x0 -> x18, waiting for transfers between devices: none -> 408 us  [the longest x8 408 us: other_z(): return lax.ppermute(value, 'z', SWAP)]
    dot_general x17 -> x0, matrix products: 382 us -> none  [the longest x1 46.7 us: device_step(): jnp.einsum('btd,btcf->dcf', normed2_b, grad_upgate, preferred_element_typ...]
    all_gather x4, waiting for transfers between devices: 264 us -> 58.6 us  [gather(): return lax.all_gather(weight, ('c', 'y', 'x'), axis=axis, tiled=True)]
    reduce_sum x6 -> x0, other arithmetic: 24.7 us -> none  [the longest x2 11.6 us: norm_backward(): grad_mean = jnp.mean(grad_norm, axis=-1, keepdims=True)]
  transfers between devices with their start and end apart: 11 -> 26, of which waited for: 10 -> 13; matrix products, arithmetic and copies ran while one was open for 14% -> 3% of each run, Pallas kernels for 0% -> 27%
where the time goes in v1:
time: 1300 us; the launch traced here: 1290 us
  waiting for transfers between devices  781 us (60%)
  Pallas kernels  439 us (34%)
  local copies, waits for them, and re-layouts  32.2 us (2%)
  between operations  14.4 us (1%)
  starting transfers between devices  13.3 us (1%)
    pallas_call x27, Pallas kernels, call(): pl.pallas_call(kernel, out_shape=out_shape, grid_spec=pltpu.PrefetchScala...  439 us
    ppermute x8, waiting for transfers between devices, other_z(): return lax.ppermute(value, 'z', SWAP)  408 us
    reduce_scatter x4, waiting for transfers between devices, scatter(): lax.psum_scatter(grad, ('y', 'x'), scatter_dimension=axis, tiled=True)  311 us
    all_gather x4, waiting for transfers between devices, gather(): return lax.all_gather(weight, ('c', 'y', 'x'), axis=axis, tiled=True)  58.6 us
    unnamed x14, local copies, waits for them, and re-layouts  32.2 us
  transfers between devices with their start and end apart: 26, of which 13 were waited for; matrix products, arithmetic and copies ran while one was open for 3% of the time, Pallas kernels for 27%

profile of v1, /device:TPU:0, one launch (start us, length us, event | category | flops | bytes accessed | tf_op | source)
XLA Modules:
  0.0 1293.2 jit_solution(12675316590780584097)
XLA Ops:
  19.2 11.3 shard_map.109
  32.6 48.9 %all-gather.5.cloned.1.call-done.w_ref = bf16[2048,3072]{1,0:T(8,128)(2,1)} async-done(((bf16[256,3072]{1,0:T(8,128)(2,1)}), bf16[2048,3072]{1,0:T(8,128)(2,1)}) %all-gather.5.cloned.1.call-update) | async-done | bytes 12582928 | tf_op jit(solution)/shard_map/all_gather | solution.py:273
  81.5 22.4 %shard_map.110 = (bf16[1024,3072]{1,0:T(8,128)(2,1)}, bf16[3,1024,1024]{2,1,0:T(8,128)(2,1)}) custom-call(s32[2]{0:T(128)} %pad_add_fusion.ids, bf16[1024,2048]{1,0:T(8,128)(2,1)} %get-tuple-element.70.n1_ref.a_ref, bf16[2048,3072]{1,0:T(8,128)(2,1)} %all-gather.5.cloned.1.call-done.w_ref, f32[512,128]{1,0:T(8,128)} %get-tuple-element.83.cos_ref, ...), custom_call_target="tpu_custom_call" | custom-call | flops 12884901888 | bytes 29884416 | tf_op jit(solution)/shard_map/pallas_call | solution.py:49
  103.8 17.1 %shard_map.111.refs_0_.a_ref = bf16[1024,1024]{1,0:T(8,128)(2,1)} custom-call(s32[2]{0:T(128)} %pad_add_fusion.ids, bf16[1024,3072]{1,0:T(8,128)(2,1)} %get-tuple-element.42.q_ref.k_ref.v_ref, bf16[1024,3072]{1,0:T(8,128)(2,1)} %get-tuple-element.42.q_ref.k_ref.v_ref, bf16[1024,3072]{1,0:T(8,128)(2,1)} %get-tuple-element.42.q_ref.k_ref.v_ref), custom_call_target="tpu_custom_call" | custom-call | flops 2147483648 | bytes 20971520 | tf_op jit(solution)/shard_map/pallas_call | solution.py:49
  137.5 84.1 %collective-permute-done.recv_ref = f32[512,2048]{1,0:T(8,128)} collective-permute-done((f32[512,2048]{1,0:T(8,128)}, f32[512,2048]{1,0:T(8,128)}, u32[]{:S(2)}, u32[]{:S(2)}) %collective-permute-start) | collective-permute-done | bytes 4194336 | tf_op jit(solution)/shard_map/ppermute | solution.py:261
  230.4 45.7 %collective-permute-done.1.theirs_ref = bf16[512,2048]{1,0:T(8,128)(2,1)S(1)} collective-permute-done((bf16[512,2048]{1,0:T(8,128)(2,1)}, bf16[512,2048]{1,0:T(8,128)(2,1)S(1)}, u32[]{:S(2)}, u32[]{:S(2)}) %collective-permute-start.1) | collective-permute-done | bytes 2097184 | tf_op jit(solution)/shard_map/ppermute | solution.py:261
  277.4 24.8 %shard_map.115 = (f32[1024,2048]{1,0:T(8,128)}, f32[1024,2048]{1,0:T(8,128)}, bf16[1024,2048]{1,0:T(8,128)(2,1)}, bf16[1024,2048]{1,0:T(8,128)(2,1)}) custom-call(s32[2]{0:T(128)} %pad_add_fusion.ids, bf16[512,2048]{1,0:T(8,128)(2,1)} %copy-done.3, bf16[512,2048]{1,0:T(8,128)(2,1)} %get-tuple-element.46.mine_ref, ...), custom_call_target="tpu_custom_call" | custom-call | flops 17179869184 | bytes 96468992 | tf_op jit(solution)/shard_map/pallas_call | solution.py:49
  302.2 25.3 %shard_map.116 = (f32[1024,2048]{1,0:T(8,128)}, f32[1024,2048]{1,0:T(8,128)}, bf16[1024,2048]{1,0:T(8,128)(2,1)}, bf16[1024,2048]{1,0:T(8,128)(2,1)}) custom-call(s32[2]{0:T(128)} %pad_add_fusion.ids, bf16[512,2048]{1,0:T(8,128)(2,1)} %copy-done.3, bf16[512,2048]{1,0:T(8,128)(2,1)} %get-tuple-element.46.mine_ref, ...), custom_call_target="tpu_custom_call" | custom-call | flops 17179869184 | bytes 96468992 | tf_op jit(solution)/shard_map/pallas_call | solution.py:49
  328.0 14.4 %shard_map.117.rest_0_ = f32[4,4096,256]{2,1,0:T(8,128)} custom-call(s32[2]{0:T(128)} %pad_add_fusion.ids, bf16[1024,2048]{1,0:T(8,128)(2,1)} %get-tuple-element.63.a_ref.refs_0_, bf16[1024,2048]{1,0:T(8,128)(2,1)} %collective-permute-done.5.a2_ref, bf16[1024,2048]{1,0:T(8,128)(2,1)} %get-tuple-element.60.b_ref.gy_ref, ...), custom_call_target="tpu_custom_call" | custom-call | flops 8589934592 | bytes 33554432 | tf_op jit(solution)/shard_map/pallas_call | solution.py:49
  342.4 14.7 %shard_map.118 = f32[4,4096,256]{2,1,0:T(8,128)} custom-call(s32[2]{0:T(128)} %pad_add_fusion.ids, bf16[1024,2048]{1,0:T(8,128)(2,1)} %get-tuple-element.50.a_ref.refs_1_, bf16[1024,2048]{1,0:T(8,128)(2,1)} %collective-permute-done.3.a2_ref, bf16[1024,2048]{1,0:T(8,128)(2,1)} %get-tuple-element.60.b_ref.gy_ref, ...), custom_call_target="tpu_custom_call", output_to_operand_aliasing={{}: (5, {})} | custom-call | flops 8589934592 | bytes 50331648 | tf_op jit(solution)/shard_map/pallas_call | solution.py:49
  366.8 19.9 %shard_map.119.lo_ref.b_ref = bf16[2,1024,2048]{2,1,0:T(8,128)(2,1)} custom-call(s32[2]{0:T(128)} %pad_add_fusion.ids, bf16[1024,2048]{1,0:T(8,128)(2,1)} %get-tuple-element.60.b_ref.gy_ref, bf16[4096,2048]{1,0:T(8,128)(2,1)} %all-gather.11.cloned.1.call-done.w_ref.refs_2_, f32[1024,2048]{1,0:T(8,128)} %get-tuple-element.53.u_ref, ...), custom_call_target="tpu_custom_call" | custom-call | flops 8589934592 | bytes 46137344 | tf_op jit(solution)/shard_map/pallas_call | solution.py:49
  387.0 19.6 %shard_map.120.hi_ref.b_ref = bf16[2,1024,2048]{2,1,0:T(8,128)(2,1)} custom-call(s32[2]{0:T(128)} %pad_add_fusion.ids, bf16[1024,2048]{1,0:T(8,128)(2,1)} %get-tuple-element.60.b_ref.gy_ref, bf16[4096,2048]{1,0:T(8,128)(2,1)} %all-gather.11.cloned.1.call-done.w_ref.refs_2_, f32[1024,2048]{1,0:T(8,128)} %get-tuple-element.56.u_ref, ...), custom_call_target="tpu_custom_call" | custom-call | flops 8589934592 | bytes 46137344 | tf_op jit(solution)/shard_map/pallas_call | solution.py:49
  407.1 25.4 %shard_map.121 = f32[512,2048]{1,0:T(8,128)} custom-call(s32[2]{0:T(128)} %pad_add_fusion.ids, bf16[2,1024,2048]{2,1,0:T(8,128)(2,1)} %shard_map.119.lo_ref.b_ref, bf16[2,1024,2048]{2,1,0:T(8,128)(2,1)} %shard_map.120.hi_ref.b_ref, bf16[2,2048,4096]{2,1,0:T(8,128)(2,1)} %all-gather.9.cloned.1.call-done.wu_ref.wg_ref.w_ref), custom_call_target="tpu_custom_call" | custom-call | flops 17179869184 | bytes 54525952 | tf_op jit(solution)/shard_map/pallas_call | solution.py:49
  433.9 25.3 %shard_map.122.part_ref = f32[512,2048]{1,0:T(8,128)} custom-call(s32[2]{0:T(128)} %pad_add_fusion.ids, bf16[2,1024,2048]{2,1,0:T(8,128)(2,1)} %shard_map.119.lo_ref.b_ref, bf16[2,1024,2048]{2,1,0:T(8,128)(2,1)} %shard_map.120.hi_ref.b_ref, bf16[2,2048,4096]{2,1,0:T(8,128)(2,1)} %all-gather.9.cloned.1.call-done.wu_ref.wg_ref.w_ref), custom_call_target="tpu_custom_call" | custom-call | flops 17179869184 | bytes 54525952 | tf_op jit(solution)/shard_map/pallas_call | solution.py:49
  459.2 25.1 %shard_map.123.rest_0_ = f32[2,1024,4096]{2,1,0:T(8,128)} custom-call(s32[2]{0:T(128)} %pad_add_fusion.ids, bf16[1024,2048]{1,0:T(8,128)(2,1)} %get-tuple-element.59.a_ref, bf16[1024,2048]{1,0:T(8,128)(2,1)} %collective-permute-done.2.a2_ref, bf16[2,1024,2048]{2,1,0:T(8,128)(2,1)} %shard_map.119.lo_ref.b_ref, ...), custom_call_target="tpu_custom_call" | custom-call | flops 17179869184 | bytes 58720256 | tf_op jit(solution)/shard_map/pallas_call | solution.py:49
  484.3 25.4 %shard_map.124 = f32[2,1024,4096]{2,1,0:T(8,128)} custom-call(s32[2]{0:T(128)} %pad_add_fusion.ids, bf16[1024,2048]{1,0:T(8,128)(2,1)} %get-tuple-element.59.a_ref, bf16[1024,2048]{1,0:T(8,128)(2,1)} %collective-permute-done.2.a2_ref, bf16[2,1024,2048]{2,1,0:T(8,128)(2,1)} %shard_map.120.hi_ref.b_ref, ...), custom_call_target="tpu_custom_call", output_to_operand_aliasing={{}: (5, {})} | custom-call | flops 17179869184 | bytes 92274688 | tf_op jit(solution)/shard_map/pallas_call | solution.py:49
  509.7 15.8 %collective-permute-done.8.recv_ref = f32[512,2048]{1,0:T(8,128)} collective-permute-done((f32[512,2048]{1,0:T(8,128)}, f32[512,2048]{1,0:T(8,128)}, u32[]{:S(2)}, u32[]{:S(2)}) %collective-permute-start.8) | collective-permute-done | bytes 4194336 | tf_op jit(solution)/shard_map/ppermute | solution.py:261
  536.2 14.8 %shard_map.126 = f32[512,2048]{1,0:T(8,128)} custom-call(s32[2]{0:T(128)} %pad_add_fusion.ids, bf16[1024,2048]{1,0:T(8,128)(2,1)} %get-tuple-element.63.a_ref.refs_0_, bf16[1024,2048]{1,0:T(8,128)(2,1)} %get-tuple-element.50.a_ref.refs_1_, bf16[4096,2048]{1,0:T(8,128)(2,1)} %all-gather.11.cloned.1.call-done.w_ref.refs_2_), custom_call_target="tpu_custom_call" | custom-call | flops 8589934592 | bytes 29360128 | tf_op jit(solution)/shard_map/pallas_call | solution.py:49
  551.0 14.8 %shard_map.127.part_ref = f32[512,2048]{1,0:T(8,128)} custom-call(s32[2]{0:T(128)} %pad_add_fusion.ids, bf16[1024,2048]{1,0:T(8,128)(2,1)} %get-tuple-element.63.a_ref.refs_0_, bf16[1024,2048]{1,0:T(8,128)(2,1)} %get-tuple-element.50.a_ref.refs_1_, bf16[4096,2048]{1,0:T(8,128)(2,1)} %all-gather.11.cloned.1.call-done.w_ref.refs_2_), custom_call_target="tpu_custom_call" | custom-call | flops 8589934592 | bytes 29360128 | tf_op jit(solution)/shard_map/pallas_call | solution.py:49
  565.7 16.1 %collective-permute-done.9.theirs_ref = bf16[512,2048]{1,0:T(8,128)(2,1)S(1)} collective-permute-done((bf16[512,2048]{1,0:T(8,128)(2,1)}, bf16[512,2048]{1,0:T(8,128)(2,1)S(1)}, u32[]{:S(2)}, u32[]{:S(2)}) %collective-permute-start.9) | collective-permute-done | bytes 2097184 | tf_op jit(solution)/shard_map/ppermute | solution.py:261
  592.8 26.4 %shard_map.129.d_ref.b_ref = bf16[3,1024,1024]{2,1,0:T(8,128)(2,1)} custom-call(s32[2]{0:T(128)} %pad_add_fusion.ids, bf16[1024,3072]{1,0:T(8,128)(2,1)} %get-tuple-element.42.q_ref.k_ref.v_ref, bf16[1024,3072]{1,0:T(8,128)(2,1)} %get-tuple-element.42.q_ref.k_ref.v_ref, bf16[1024,3072]{1,0:T(8,128)(2,1)} %get-tuple-element.42.q_ref.k_ref.v_ref, ...), custom_call_target="tpu_custom_call" | custom-call | flops 5368709120 | bytes 34078720 | tf_op jit(solution)/shard_map/pallas_call | solution.py:49
  620.2 12.4 shard_map.130
  632.6 12.6 shard_map.131.part_ref
  654.9 20.4 %shard_map.133 = f32[1024,3072]{1,0:T(8,128)} custom-call(s32[2]{0:T(128)} %pad_add_fusion.ids, bf16[1024,2048]{1,0:T(8,128)(2,1)} %get-tuple-element.70.n1_ref.a_ref, bf16[1024,2048]{1,0:T(8,128)(2,1)} %collective-permute-done.12.a2_ref, bf16[3,1024,1024]{2,1,0:T(8,128)(2,1)} %shard_map.129.d_ref.b_ref, bf16[3,1024,1024]{2,1,0:T(8,128)(2,1)} %collective-permute-done.13.b2_ref), custom_call_target="tpu_custom_call" | custom-call | flops 12884901888 | bytes 33554432 | tf_op jit(solution)/shard_map/pallas_call | solution.py:49
  679.5 91.7 %collective-permute-done.14.recv_ref = f32[512,2048]{1,0:T(8,128)} collective-permute-done((f32[512,2048]{1,0:T(8,128)}, f32[512,2048]{1,0:T(8,128)}, u32[]{:S(2)}, u32[]{:S(2)}) %collective-permute-start.14) | collective-permute-done | bytes 4194336 | tf_op jit(solution)/shard_map/ppermute | solution.py:261
  779.5 81.6 %collective-permute-done.16.recv_ref = f32[512,2048]{1,0:T(8,128)} collective-permute-done((f32[512,2048]{1,0:T(8,128)}, f32[512,2048]{1,0:T(8,128)}, u32[]{:S(2)}, u32[]{:S(2)}) %collective-permute-start.16) | collective-permute-done | bytes 4194336 | tf_op jit(solution)/shard_map/ppermute | solution.py:261
  871.6 34.5 %collective-permute-done.15 = bf16[512,2048]{1,0:T(8,128)(2,1)} collective-permute-done((bf16[512,2048]{1,0:T(8,128)(2,1)}, bf16[512,2048]{1,0:T(8,128)(2,1)}, u32[]{:S(2)}, u32[]{:S(2)}) %collective-permute-start.15) | collective-permute-done | bytes 2097184 | tf_op jit(solution)/shard_map/ppermute | solution.py:261
  911.4 38.7 %collective-permute-done.17 = bf16[512,2048]{1,0:T(8,128)(2,1)} collective-permute-done((bf16[512,2048]{1,0:T(8,128)(2,1)}, bf16[512,2048]{1,0:T(8,128)(2,1)}, u32[]{:S(2)}, u32[]{:S(2)}) %collective-permute-start.17) | collective-permute-done | bytes 2097184 | tf_op jit(solution)/shard_map/ppermute | solution.py:261
  959.4 120.7 %reduce-scatter.9.cloned.1.call-done = f32[2,256,4096]{2,1,0:T(8,128)} async-done(((f32[2,1024,4096]{2,1,0:T(8,128)}), f32[2,256,4096]{2,1,0:T(8,128)}) %reduce-scatter.9.cloned.1.call-update) | async-done | bytes 8388624 | tf_op jit(solution)/shard_map/reduce_scatter | solution.py:277
  1080.1 15.4 %copy.15 = f32[256,2,4096]{2,1,0:T(2,128)} copy(f32[256,2,4096]{2,0,1:T(8,128)} %bitcast.25) | data formatting | bytes 16777216
  1095.5 37.0 %reduce-scatter.7.cloned.1.call-done = f32[1024,256]{1,0:T(8,128)} async-done(((f32[4096,256]{1,0:T(8,128)}), f32[1024,256]{1,0:T(8,128)}) %reduce-scatter.7.cloned.1.call-update) | async-done | bytes 1048592 | tf_op jit(solution)/shard_map/reduce_scatter | solution.py:277
  1132.5 153.6 %reduce-scatter.11.cloned.1.call-done = f32[4096,256]{1,0:T(8,128)} async-done(((f32[16384,256]{1,0:T(8,128)}), f32[4096,256]{1,0:T(8,128)}) %reduce-scatter.11.cloned.1.call-update) | async-done | bytes 4194320 | tf_op jit(solution)/shard_map/reduce_scatter | solution.py:277
  (75 shorter events, 122.8 us)
Async XLA Ops:
  7.2 74.3 %all-gather.5.cloned.1.call-start = ((), (), s32[]{:S(2)}) async-start(), calls=%async_computation.4 | async-start | bytes 14155776 | tf_op jit(solution)/shard_map/all_gather | solution.py:273
  10.1 110.8 %all-gather.7.cloned.1.call-start = ((), (), s32[]{:S(2)}) async-start(), calls=%async_computation.5 | async-start | bytes 4718592 | tf_op jit(solution)/shard_map/all_gather | solution.py:273
  10.9 265.2 %all-gather.9.cloned.1.call-start = ((), (), s32[]{:S(2)}) async-start(), calls=%async_computation.6 | async-start | bytes 37748736 | tf_op jit(solution)/shard_map/all_gather | solution.py:273
  18.0 348.8 %all-gather.11.cloned.1.call-start = ((), (), s32[]{:S(2)}) async-start(), calls=%async_computation.7 | async-start | bytes 18874368 | tf_op jit(solution)/shard_map/all_gather | solution.py:273
  18.6 936.6 %reduce-scatter.5.cloned.1.call-start = ((), (), s32[]{:S(2)}) async-start(), calls=%async_computation.8 | async-start | bytes 15728640 | tf_op jit(solution)/shard_map/reduce_scatter | solution.py:277
  128.6 93.0 %collective-permute-start = (f32[512,2048]{1,0:T(8,128)}, f32[512,2048]{1,0:T(8,128)}, u32[]{:S(2)}, u32[]{:S(2)}) collective-permute-start(f32[512,2048]{1,0:T(8,128)} %shard_map.112), channel_id=1, source_target_pairs={{0,8},{8,0},{1,9},{9,1},{2,10},{10,2},{3,11},{11,3},{4,12},{12,4},... | collective-permute-start | bytes 12582920 | tf_op jit(solution)/shard_map/ppermute | solution.py:261
  229.0 47.1 %collective-permute-start.1 = (bf16[512,2048]{1,0:T(8,128)(2,1)}, bf16[512,2048]{1,0:T(8,128)(2,1)S(1)}, u32[]{:S(2)}, u32[]{:S(2)}) collective-permute-start(bf16[512,2048]{1,0:T(8,128)(2,1)} %get-tuple-element.46.mine_ref), channel_id=1, source_target_pairs={{0,8},{8,0},{1,9},{9,1},{2,10},{10,2},{3,11},{11,3},{4,12},{12,4},... | collective-permute-start | bytes 6291464 | tf_op jit(solution)/shard_map/ppermute | solution.py:261
  230.4 97.6 %collective-permute-start.4 = (bf16[1024,2048]{1,0:T(8,128)(2,1)}, bf16[1024,2048]{1,0:T(8,128)(2,1)}, u32[]{:S(2)}, u32[]{:S(2)}) collective-permute-start(bf16[1024,2048]{1,0:T(8,128)(2,1)} %get-tuple-element.60.b_ref.gy_ref), channel_id=1, source_target_pairs={{0,1},{1,0},{2,3},{3,2},{4,5},{5,4},{6,7},{7,6},{8,9},{9,8},{10,11... | collective-permute-start | bytes 12582920 | tf_op jit(solution)/shard_map/ppermute | solution.py:265
  276.1 1.3 copy-start.3
  302.2 25.8 %collective-permute-start.5 = (bf16[1024,2048]{1,0:T(8,128)(2,1)}, bf16[1024,2048]{1,0:T(8,128)(2,1)}, u32[]{:S(2)}, u32[]{:S(2)}) collective-permute-start(bf16[1024,2048]{1,0:T(8,128)(2,1)} %get-tuple-element.63.a_ref.refs_0_), channel_id=1, source_target_pairs={{0,1},{1,0},{2,3},{3,2},{4,5},{5,4},{6,7},{7,6},{8,9},{9,8},{10,11... | collective-permute-start | bytes 12582920 | tf_op jit(solution)/shard_map/ppermute | solution.py:265
  327.5 14.9 %collective-permute-start.3 = (bf16[1024,2048]{1,0:T(8,128)(2,1)}, bf16[1024,2048]{1,0:T(8,128)(2,1)}, u32[]{:S(2)}, u32[]{:S(2)}) collective-permute-start(bf16[1024,2048]{1,0:T(8,128)(2,1)} %get-tuple-element.50.a_ref.refs_1_), channel_id=1, source_target_pairs={{0,1},{1,0},{2,3},{3,2},{4,5},{5,4},{6,7},{7,6},{8,9},{9,8},{10,11... | collective-permute-start | bytes 12582920 | tf_op jit(solution)/shard_map/ppermute | solution.py:265
  386.7 72.5 %collective-permute-start.7 = (bf16[2,1024,2048]{2,1,0:T(8,128)(2,1)}, bf16[2,1024,2048]{2,1,0:T(8,128)(2,1)}, u32[]{:S(2)}, u32[]{:S(2)}) collective-permute-start(bf16[2,1024,2048]{2,1,0:T(8,128)(2,1)} %shard_map.119.lo_ref.b_ref), channel_id=1, source_target_pairs={{0,1},{1,0},{2,3},{3,2},{4,5},{5,4},{6,7},{7,6},{8,9},{9,8},{10,11... | collective-permute-start | bytes 25165832 | tf_op jit(solution)/shard_map/ppermute | solution.py:265
  406.6 77.7 %collective-permute-start.6 = (bf16[2,1024,2048]{2,1,0:T(8,128)(2,1)}, bf16[2,1024,2048]{2,1,0:T(8,128)(2,1)}, u32[]{:S(2)}, u32[]{:S(2)}) collective-permute-start(bf16[2,1024,2048]{2,1,0:T(8,128)(2,1)} %shard_map.120.hi_ref.b_ref), channel_id=1, source_target_pairs={{0,1},{1,0},{2,3},{3,2},{4,5},{5,4},{6,7},{7,6},{8,9},{9,8},{10,11... | collective-permute-start | bytes 25165832 | tf_op jit(solution)/shard_map/ppermute | solution.py:265
  406.8 52.4 %collective-permute-start.2 = (bf16[1024,2048]{1,0:T(8,128)(2,1)}, bf16[1024,2048]{1,0:T(8,128)(2,1)}, u32[]{:S(2)}, u32[]{:S(2)}) collective-permute-start(bf16[1024,2048]{1,0:T(8,128)(2,1)} %get-tuple-element.59.a_ref), channel_id=1, source_target_pairs={{0,1},{1,0},{2,3},{3,2},{4,5},{5,4},{6,7},{7,6},{8,9},{9,8},{10,11... | collective-permute-start | bytes 12582920 | tf_op jit(solution)/shard_map/ppermute | solution.py:265
  432.4 93.0 %collective-permute-start.8 = (f32[512,2048]{1,0:T(8,128)}, f32[512,2048]{1,0:T(8,128)}, u32[]{:S(2)}, u32[]{:S(2)}) collective-permute-start(f32[512,2048]{1,0:T(8,128)} %shard_map.121), channel_id=1, source_target_pairs={{0,8},{8,0},{1,9},{9,1},{2,10},{10,2},{3,11},{11,3},{4,12},{12,4},... | collective-permute-start | bytes 12582920 | tf_op jit(solution)/shard_map/ppermute | solution.py:261
  534.7 47.1 %collective-permute-start.9 = (bf16[512,2048]{1,0:T(8,128)(2,1)}, bf16[512,2048]{1,0:T(8,128)(2,1)S(1)}, u32[]{:S(2)}, u32[]{:S(2)}) collective-permute-start(bf16[512,2048]{1,0:T(8,128)(2,1)} %get-tuple-element.64.mine_ref), channel_id=1, source_target_pairs={{0,8},{8,0},{1,9},{9,1},{2,10},{10,2},{3,11},{11,3},{4,12},{12,4},... | collective-permute-start | bytes 6291464 | tf_op jit(solution)/shard_map/ppermute | solution.py:261
  581.8 1.3 copy-start.4
  592.8 27.0 %copy-start = (bf16[1024,1024]{1,0:T(8,128)(2,1)S(1)}, bf16[1024,1024]{1,0:T(8,128)(2,1)}, u32[]{:S(2)}) copy-start(bf16[1024,1024]{1,0:T(8,128)(2,1)} %shard_map.111.refs_0_.a_ref) | copy-start | bytes 6291460
  619.2 35.8 %collective-permute-start.13 = (bf16[3,1024,1024]{2,1,0:T(8,128)(2,1)}, bf16[3,1024,1024]{2,1,0:T(8,128)(2,1)}, u32[]{:S(2)}, u32[]{:S(2)}) collective-permute-start(bf16[3,1024,1024]{2,1,0:T(8,128)(2,1)} %shard_map.129.d_ref.b_ref), channel_id=1, source_target_pairs={{0,1},{1,0},{2,3},{3,2},{4,5},{5,4},{6,7},{7,6},{8,9},{9,8},{10,11... | collective-permute-start | bytes 18874376 | tf_op jit(solution)/shard_map/ppermute | solution.py:265
  619.2 26.1 %collective-permute-start.11 = (bf16[1024,2048]{1,0:T(8,128)(2,1)}, bf16[1024,2048]{1,0:T(8,128)(2,1)}, u32[]{:S(2)}, u32[]{:S(2)}) collective-permute-start(bf16[1024,2048]{1,0:T(8,128)(2,1)} %get-tuple-element.69.b_ref), channel_id=1, source_target_pairs={{0,1},{1,0},{2,3},{3,2},{4,5},{5,4},{6,7},{7,6},{8,9},{9,8},{10,11... | collective-permute-start | bytes 12582920 | tf_op jit(solution)/shard_map/ppermute | solution.py:265
  619.7 35.2 %collective-permute-start.12 = (bf16[1024,2048]{1,0:T(8,128)(2,1)}, bf16[1024,2048]{1,0:T(8,128)(2,1)}, u32[]{:S(2)}, u32[]{:S(2)}) collective-permute-start(bf16[1024,2048]{1,0:T(8,128)(2,1)} %get-tuple-element.70.n1_ref.a_ref), channel_id=1, source_target_pairs={{0,1},{1,0},{2,3},{3,2},{4,5},{5,4},{6,7},{7,6},{8,9},{9,8},{10,11... | collective-permute-start | bytes 12582920 | tf_op jit(solution)/shard_map/ppermute | solution.py:265
  619.7 25.5 %collective-permute-start.10 = (bf16[1024,1024]{1,0:T(8,128)(2,1)S(1)}, bf16[1024,1024]{1,0:T(8,128)(2,1)}, u32[]{:S(2)}, u32[]{:S(2)}) collective-permute-start(bf16[1024,1024]{1,0:T(8,128)(2,1)S(1)} %copy-done), channel_id=1, source_target_pairs={{0,1},{1,0},{2,3},{3,2},{4,5},{5,4},{6,7},{7,6},{8,9},{9,8},{10,11... | collective-permute-start | bytes 6291464 | tf_op jit(solution)/shard_map/ppermute | solution.py:265
  675.4 404.7 %reduce-scatter.9.cloned.1.call-start = ((), (), s32[]{:S(2)}) async-start(), calls=%async_computation.10 | async-start | bytes 41943040 | tf_op jit(solution)/shard_map/reduce_scatter | solution.py:277
  676.0 456.6 %reduce-scatter.7.cloned.1.call-start = ((), (), s32[]{:S(2)}) async-start(), calls=%async_computation.9 | async-start | bytes 5242880 | tf_op jit(solution)/shard_map/reduce_scatter | solution.py:277
  676.7 609.4 %reduce-scatter.11.cloned.1.call-start = ((), (), s32[]{:S(2)}) async-start(), calls=%async_computation.11 | async-start | bytes 20971520 | tf_op jit(solution)/shard_map/reduce_scatter | solution.py:277
  677.5 93.8 %collective-permute-start.14 = (f32[512,2048]{1,0:T(8,128)}, f32[512,2048]{1,0:T(8,128)}, u32[]{:S(2)}, u32[]{:S(2)}) collective-permute-start(f32[512,2048]{1,0:T(8,128)} %shard_map.126), channel_id=1, source_target_pairs={{0,8},{8,0},{1,9},{9,1},{2,10},{10,2},{3,11},{11,3},{4,12},{12,4},... | collective-permute-start | bytes 12582920 | tf_op jit(solution)/shard_map/ppermute | solution.py:261
  679.0 182.2 %collective-permute-start.16 = (f32[512,2048]{1,0:T(8,128)}, f32[512,2048]{1,0:T(8,128)}, u32[]{:S(2)}, u32[]{:S(2)}) collective-permute-start(f32[512,2048]{1,0:T(8,128)} %shard_map.130), channel_id=1, source_target_pairs={{0,8},{8,0},{1,9},{9,1},{2,10},{10,2},{3,11},{11,3},{4,12},{12,4},... | collective-permute-start | bytes 12582920 | tf_op jit(solution)/shard_map/ppermute | solution.py:261
  778.1 128.0 %collective-permute-start.15 = (bf16[512,2048]{1,0:T(8,128)(2,1)}, bf16[512,2048]{1,0:T(8,128)(2,1)}, u32[]{:S(2)}, u32[]{:S(2)}) collective-permute-start(bf16[512,2048]{1,0:T(8,128)(2,1)} %shard_map.134), channel_id=1, source_target_pairs={{0,8},{8,0},{1,9},{9,1},{2,10},{10,2},{3,11},{11,3},{4,12},{12,4},... | collective-permute-start | bytes 6291464 | tf_op jit(solution)/shard_map/ppermute | solution.py:261
  779.5 126.6 %copy-start.1 = (bf16[512,2048]{1,0:T(8,128)(2,1)S(1)}, bf16[512,2048]{1,0:T(8,128)(2,1)}, u32[]{:S(2)}) copy-start(bf16[512,2048]{1,0:T(8,128)(2,1)} %shard_map.134) | copy-start | bytes 6291460
  870.2 80.0 %collective-permute-start.17 = (bf16[512,2048]{1,0:T(8,128)(2,1)}, bf16[512,2048]{1,0:T(8,128)(2,1)}, u32[]{:S(2)}, u32[]{:S(2)}) collective-permute-start(bf16[512,2048]{1,0:T(8,128)(2,1)} %shard_map.135), channel_id=1, source_target_pairs={{0,8},{8,0},{1,9},{9,1},{2,10},{10,2},{3,11},{11,3},{4,12},{12,4},... | collective-permute-start | bytes 6291464 | tf_op jit(solution)/shard_map/ppermute | solution.py:261
  871.6 78.5 %copy-start.2 = (bf16[512,2048]{1,0:T(8,128)(2,1)S(1)}, bf16[512,2048]{1,0:T(8,128)(2,1)}, u32[]{:S(2)}) copy-start(bf16[512,2048]{1,0:T(8,128)(2,1)} %shard_map.135) | copy-start | bytes 6291460
Sparse Core Ops, SparseCore 0:
  10.4 71.0 all-gather.4
  83.3 33.6 all-gather.6
  118.8 156.8 all-gather.8
  277.5 89.2 all-gather.10
  675.5 116.8 reduce-scatter.4
  795.3 284.7 reduce-scatter.8
  1083.6 48.8 reduce-scatter.6
  1136.1 149.9 reduce-scatter.10

commit v2 on v1

v2 whole, which is shorter than its diff:
```python
import functools

import jax
import jax.numpy as jnp
import numpy as np
from jax import lax
from jax.experimental import pallas as pl
from jax.experimental.pallas import tpu as pltpu
from jax.sharding import Mesh, PartitionSpec as P


F32 = jnp.float32
BF16 = jnp.bfloat16
SWAP = [(0, 1), (1, 0)]
EPS = 1e-5
CLIP = 8.0
SHARD = 256
ROLES = 14
OWN_ROLES = (0, 4, 1, 3, 6, 7)


VMEM_LIMIT = 60 * 1024 * 1024


def dot_nn(a, b):
    return lax.dot_general(a, b, (((1,), (0,)), ((), ())), preferred_element_type=F32)


def dot_nt(a, b):
    return lax.dot_general(a, b, (((1,), (1,)), ((), ())), preferred_element_type=F32)


def dot_tn(a, b):
    return lax.dot_general(a, b, (((0,), (0,)), ((), ())), preferred_element_type=F32)


def norm_stats(values):
    mean_val = jnp.mean(values, axis=-1, keepdims=True)
    centered = values - mean_val
    inv_std = lax.rsqrt(jnp.mean(centered * centered, axis=-1, keepdims=True) + EPS)
    return centered * inv_std, inv_std


def norm_backward(grad_norm, normed, inv_std):
    grad_mean = jnp.mean(grad_norm, axis=-1, keepdims=True)
    proj_mean = jnp.mean(grad_norm * normed, axis=-1, keepdims=True)
    return inv_std * (grad_norm - grad_mean - normed * proj_mean)


def call(kernel, grid, in_specs, out_specs, out_shape, ids, operands, flops, scratch=(), aliases=None, collective=None):
    nbytes = sum(int(np.prod(o.shape)) * o.dtype.itemsize for o in operands)
    nbytes += sum(int(np.prod(o.shape)) * o.dtype.itemsize for o in jax.tree.leaves(out_shape))
    return pl.pallas_call(
        kernel,
        out_shape=out_shape,
        grid_spec=pltpu.PrefetchScalarGridSpec(
            num_scalar_prefetch=0 if ids is None else 1, grid=grid, in_specs=in_specs, out_specs=out_specs, scratch_shapes=scratch
        ),
        input_output_aliases=aliases or {},
        compiler_params=pltpu.CompilerParams(
            dimension_semantics=('arbitrary',) * len(grid), vmem_limit_bytes=VMEM_LIMIT,
            collective_id=collective, has_side_effects=collective is not None,
        ),
        cost_estimate=pl.CostEstimate(flops=int(flops), bytes_accessed=int(nbytes), transcendentals=0),
    )(*([] if ids is None else [ids]), *operands)


def sds(shape, dtype):
    return jax.ShapeDtypeStruct(shape, dtype)


def column_order(block, width):
    n = width // SHARD
    return [block[:, s * SHARD:(s + 1) * SHARD] for s in list(range(0, n, 2)) + list(range(1, n, 2))]


class PlaneGather:
    def __init__(self, own, place, send_sem, recv_sem):
        y, x, core = lax.axis_index('y'), lax.axis_index('x'), lax.axis_index('c')
        self.targets = ({'x': 1 - x}, {'y': 1 - y}, {'c': 1 - core})
        self.own, self.send_sem, self.recv_sem = own, send_sem, recv_sem
        self.place = lambda flip_y, flip_x, h: place(core * 4 + (1 - y if flip_y else y) * 2 + (1 - x if flip_x else x), h)

    def copy(self, role):
        to_x, to_y, to_core = self.targets
        if role < 2:
            src, dst, target = self.own(role), self.place(0, 0, role), to_x
        elif role == 2:
            src, dst, target = self.place(1, 0, 1), self.place(1, 0, 1), to_x
        elif role < 5:
            src, dst, target = self.own(role - 3), self.place(0, 0, role - 3), to_y
        elif role == 5:
            src, dst, target = self.place(0, 1, 0), self.place(0, 1, 0), to_y
        elif role < 8:
            src, dst, target = self.own(role - 6), self.place(0, 0, role - 6), to_core
        else:
            flip_y, flip_x = ((0, 1), (1, 0), (1, 1))[(role - 8) // 2]
            src, dst, target = self.place(flip_y, flip_x, role % 2), self.place(flip_y, flip_x, role % 2), to_core
        return pltpu.make_async_remote_copy(src, dst, self.send_sem.at[role], self.recv_sem.at[role], device_id=target,
                                            device_id_type=pl.DeviceIdType.MESH)

    def meet(self):
        barrier = pltpu.get_barrier_semaphore()
        for target in self.targets:
            pl.semaphore_signal(barrier, inc=1, device_id=target, device_id_type=pl.DeviceIdType.MESH)
        pl.semaphore_wait(barrier, 3)

    def start(self):
        for role in OWN_ROLES:
            self.copy(role).start()

    def pass_on(self, pairs):
        for arrived, onward in pairs:
            self.copy(arrived).wait_recv()
            for role in onward:
                self.copy(role).start()

    def first(self):
        self.pass_on(((0, (5, 8)), (4, (2, 11))))

    def rest(self):
        self.pass_on(((1, (9,)), (3, (10,)), (5, (12,)), (2, (13,))))

    def finish(self):
        for role in range(6, ROLES):
            self.copy(role).wait_recv()
        for role in range(ROLES):
            self.copy(role).wait_send()


def q_gather(own_ref, full_ref, send_sem, recv_sem):
    n = own_ref.shape[0] // 2
    place = lambda shard, h: full_ref.at[pl.ds(pl.multiple_of((shard * 2 + h) * n, n), n)]
    return PlaneGather(lambda h: own_ref.at[pl.ds(h * n, n)], place, send_sem, recv_sem)


def o_gather(own_ref, full_ref, send_sem, recv_sem):
    n, cols = own_ref.shape[0] // 2, own_ref.shape[1]
    place = lambda shard, h: full_ref.at[shard // 4, pl.ds(h * n, n), pl.ds(pl.multiple_of(shard % 4 * cols, cols), cols)]
    return PlaneGather(lambda h: own_ref.at[pl.ds(h * n, n)], place, send_sem, recv_sem)


def own_shard():
    return lax.axis_index('c') * 4 + lax.axis_index('y') * 2 + lax.axis_index('x')


def head_kernel(x_ref, gy_ref, wf_ref, wq_ref, wo_ref, n1_ref, xp_ref, gyp_ref, ff_ref, q_full, o_full, wq_v, wo_v, local_sem, send_sem, recv_sem):
    step = pl.program_id(0)
    q_plan = q_gather(wq_ref, q_full, send_sem.at[0], recv_sem.at[0])
    o_plan = o_gather(wo_ref, o_full, send_sem.at[1], recv_sem.at[1])
    rows, cols = wq_ref.shape[0], wo_ref.shape[1]
    shard = own_shard()
    loads = [pltpu.make_async_copy(wq_ref, wq_v, local_sem.at[0]), pltpu.make_async_copy(wo_ref, wo_v, local_sem.at[1])]
    stores = [
        pltpu.make_async_copy(wq_v, q_full.at[pl.ds(pl.multiple_of(shard * rows, rows), rows)], local_sem.at[2]),
        pltpu.make_async_copy(wo_v, o_full.at[shard // 4, :, pl.ds(pl.multiple_of(shard % 4 * cols, cols), cols)], local_sem.at[3]),
    ]

    @pl.when(step == 0)
    def _():
        q_plan.meet()
        q_plan.start()
        for load in loads:
            load.start()

    values = jnp.concatenate(column_order(x_ref, x_ref.shape[1]), axis=1)
    xp_ref[...] = values
    gyp_ref[...] = jnp.concatenate(column_order(gy_ref, gy_ref.shape[1]), axis=1)
    normed, _ = norm_stats(values.astype(F32))
    n1_ref[...] = normed.astype(BF16)
    ff_ref[0] = wf_ref[:, 0, :]
    ff_ref[1] = wf_ref[:, 1, :]

    @pl.when(step == pl.num_programs(0) - 1)
    def _():
        for load, store in zip(loads, stores):
            load.wait()
            store.start()
        q_plan.first()
        o_plan.start()
        q_plan.rest()
        o_plan.first()
        o_plan.rest()
        q_plan.finish()
        o_plan.finish()
        for store in stores:
            store.wait()


def qkv_kernel(ids, n1_ref, w_ref, cos_ref, sin_ref, *rest, rotated):
    out_ref, keep_ref = rest[-2:]
    raw = dot_nn(n1_ref[...], w_ref[...])
    keep_ref[...] = (jnp.abs(raw) < CLIP).astype(BF16)
    clipped = jnp.clip(raw, -CLIP, CLIP)
    seq, head = cos_ref.shape
    rows, cols = clipped.shape

    @pl.when(pl.program_id(0) < rotated)
    def _():
        for r in range(rows // seq):
            for c in range(cols // head):
                part = clipped[r * seq:(r + 1) * seq, c * head:(c + 1) * head]
                turned = part * cos_ref[...] + pltpu.roll(part, head // 2, 1) * sin_ref[...]
                out_ref[r * seq:(r + 1) * seq, c * head:(c + 1) * head] = turned.astype(BF16)

    @pl.when(pl.program_id(0) >= rotated)
    def _():
        out_ref[...] = clipped.astype(BF16)


def softmax_rows(q, k, first_row, scale):
    s = dot_nt(q, k) * scale
    row = first_row + lax.broadcasted_iota(jnp.int32, s.shape, 0)
    col = lax.broadcasted_iota(jnp.int32, s.shape, 1)
    s = jnp.where(row >= col, s, -1e30)
    e = jnp.exp(s - jnp.max(s, axis=-1, keepdims=True))
    return e / jnp.sum(e, axis=-1, keepdims=True)


def attn_kernel(ids, q_ref, k_ref, v_ref, *rest, head, scale, rows, send):
    o_ref = rest[-1]
    seq, cols = q_ref.shape
    for c in range(cols // head):
        cs = slice(c * head, (c + 1) * head)
        for r in range(seq // rows):
            rs = slice(r * rows, (r + 1) * rows)
            ks = slice(0, (r + 1) * rows)
            p = softmax_rows(q_ref[rs, cs], k_ref[ks, cs], r * rows, scale).astype(BF16)
            o = dot_nn(p, v_ref[ks, cs]).astype(BF16)
            o_ref[rs, cs] = o
            if send:
                rest[-2][rs, cs] = o


def attn_bwd_kernel(ids, q_ref, k_ref, v_ref, do_ref, keep_ref, cos_ref, sin_ref, out_ref, dk_acc, dv_acc, *, head, scale, rows):
    seq, cols = q_ref.shape
    for c in range(cols // head):
        cs = slice(c * head, (c + 1) * head)
        for r in reversed(range(seq // rows)):
            rs = slice(r * rows, (r + 1) * rows)
            ks = slice(0, (r + 1) * rows)
            q, k, v, do = q_ref[rs, cs], k_ref[ks, cs], v_ref[ks, cs], do_ref[rs, cs]
            p = softmax_rows(q, k, r * rows, scale)
            dp = dot_nt(do, v)
            ds = (p * (dp - jnp.sum(dp * p, axis=-1, keepdims=True)) * scale).astype(BF16)
            dv = dot_tn(p.astype(BF16), do)
            dk = dot_tn(ds, q)
            dq = dot_nn(ds, k)
            dq = dq * cos_ref[rs] - pltpu.roll(dq, head // 2, 1) * sin_ref[rs]
            out_ref[0, rs, cs] = jnp.where(keep_ref[0, rs, cs] > 0, dq, 0.0).astype(BF16)
            if r == seq // rows - 1:
                dk_acc[...] = dk
                dv_acc[...] = dv
            else:
                dk_acc[ks] += dk
                dv_acc[ks] += dv
        dk = dk_acc[...]
        dk = dk * cos_ref[...] - pltpu.roll(dk, head // 2, 1) * sin_ref[...]
        out_ref[1, :, cs] = jnp.where(keep_ref[1, :, cs] > 0, dk, 0.0).astype(BF16)
        out_ref[2, :, cs] = jnp.where(keep_ref[2, :, cs] > 0, dv_acc[...], 0.0).astype(BF16)


def nn_kernel(ids, *refs):
    *a_refs, w_ref, out_ref = refs
    depth = w_ref.shape[0] // len(a_refs)
    total = dot_nn(a_refs[0][...], w_ref[0:depth])
    for i, a_ref in enumerate(a_refs[1:], 1):
        total += dot_nn(a_ref[...], w_ref[i * depth:(i + 1) * depth])
    out_ref[...] = total


def out_kernel(ids, o_ref, got_ref, w_ref, wz_ref, wc_ref, out_ref):
    total = dot_nn(o_ref[...], w_ref[...])
    first = pl.program_id(0) < pl.num_programs(0) // 2

    @pl.when(first)
    def _():
        out_ref[...] = total + dot_nn(got_ref[...], wz_ref[...])

    @pl.when(jnp.logical_not(first))
    def _():
        out_ref[...] = total + dot_nn(got_ref[...], wc_ref[...])


def combine1_kernel(ids, x_ref, part_ref, h_ref, n2_ref):
    h = (x_ref[...].astype(F32) + part_ref[...]).astype(BF16)
    h_ref[...] = h
    normed, _ = norm_stats(h.astype(F32))
    n2_ref[...] = normed.astype(BF16)


def ffn_kernel(ids, theirs_ref, mine_ref, wu_ref, wg_ref, u_ref, g_ref, act_ref, n2_ref):
    half = theirs_ref.shape[0]

    @pl.when(pl.program_id(0) == 0)
    def _():
        n2_ref[0:half] = theirs_ref[...]
        n2_ref[half:] = mine_ref[...]

    u = dot_nn(n2_ref[...], wu_ref[0])
    g = dot_nn(n2_ref[...], wg_ref[0])
    u_ref[...] = u
    g_ref[...] = g
    act_ref[...] = (g * jax.nn.sigmoid(g) * u).astype(BF16)


def dswiglu_kernel(ids, gy_ref, w_ref, u_ref, g_ref, out_ref):
    grad_act = dot_nt(gy_ref[...], w_ref[...])
    u, g = u_ref[...], g_ref[...]
    sig = jax.nn.sigmoid(g)
    out_ref[0] = (grad_act * (g * sig)).astype(BF16)
    out_ref[1] = (grad_act * u * sig * (1.0 + g * (1.0 - sig))).astype(BF16)


def grad_n2_kernel(ids, lo_ref, hi_ref, w_ref, out_ref):
    depth = lo_ref.shape[2]
    total = dot_nt(lo_ref[0], w_ref[0, :, 0:depth])
    total += dot_nt(hi_ref[0], w_ref[0, :, depth:])
    total += dot_nt(lo_ref[1], w_ref[1, :, 0:depth])
    total += dot_nt(hi_ref[1], w_ref[1, :, depth:])
    out_ref[...] = total


def combine2_kernel(ids, gy_ref, h_ref, part_ref, recv_ref, gh_ref, ghb_ref):
    normed, inv_std = norm_stats(h_ref[...].astype(F32))
    gh = gy_ref[...].astype(F32) + norm_backward(part_ref[...] + recv_ref[...], normed, inv_std)
    gh_ref[...] = gh
    ghb_ref[...] = gh.astype(BF16)


def grad_o_kernel(ids, theirs_ref, mine_ref, w_ref, out_ref):
    half, width = theirs_ref.shape
    lo, hi = slice(0, width // 2), slice(width // 2, width)
    for rows, ref in ((slice(0, half), theirs_ref), (slice(half, 2 * half), mine_ref)):
        out_ref[rows] = (dot_nt(ref[:, lo], w_ref[0]) + dot_nt(ref[:, hi], w_ref[1])).astype(BF16)


def grad_n1_kernel(ids, d_ref, w_ref, out_ref):
    depth = d_ref.shape[2]
    total = dot_nt(d_ref[0], w_ref[:, 0:depth])
    total += dot_nt(d_ref[1], w_ref[:, depth:2 * depth])
    total += dot_nt(d_ref[2], w_ref[:, 2 * depth:])
    out_ref[...] = total


def chip_columns(ref, chip, r):
    return ref[:, pl.ds(pl.multiple_of((chip ^ r) * SHARD, SHARD), SHARD)]


def put_pieces(total, axis, a1_ref, a0_ref, b1_ref, b0_ref):
    piece = [lax.slice_in_dim(total, r * SHARD, (r + 1) * SHARD, axis=axis) for r in range(4)]
    first = pl.program_id(0) < pl.num_programs(0) // 2

    @pl.when(first)
    def _():
        a1_ref[0], a1_ref[1], a0_ref[0], a0_ref[1] = piece[1], piece[3], piece[0], piece[2]

    @pl.when(jnp.logical_not(first))
    def _():
        b1_ref[0], b1_ref[1], b0_ref[0], b0_ref[1] = piece[2], piece[3], piece[0], piece[1]


def wgrad_rows_kernel(ids, t_ref, m_ref, t2_ref, m2_ref, b_ref, b2_ref, a1_ref, a0_ref, b1_ref, b0_ref, at_ref):
    n = t_ref.shape[0]

    @pl.when(pl.program_id(0) == 0)
    def _():
        for r in range(4):
            for i, ref in enumerate((t_ref, m_ref, t2_ref, m2_ref)):
                at_ref[r * SHARD:(r + 1) * SHARD, i * n:(i + 1) * n] = chip_columns(ref, ids[2], r).T

    total = dot_nn(at_ref[:, 0:2 * n], b_ref[0]) + dot_nn(at_ref[:, 2 * n:], b2_ref[0])
    put_pieces(total, 0, a1_ref, a0_ref, b1_ref, b0_ref)


def wgrad_cols_kernel(ids, a_ref, a2_ref, t_ref, m_ref, t2_ref, m2_ref, a1_ref, a0_ref, b1_ref, b0_ref, br_ref):
    n = t_ref.shape[0]

    @pl.when(pl.program_id(0) == 0)
    def _():
        for r in range(4):
            for i, ref in enumerate((t_ref, m_ref, t2_ref, m2_ref)):
                br_ref[i * n:(i + 1) * n, r * SHARD:(r + 1) * SHARD] = chip_columns(ref, ids[2], r)

    total = dot_tn(a_ref[...], br_ref[0:2 * n]) + dot_tn(a2_ref[...], br_ref[2 * n:])
    put_pieces(total, 1, a1_ref, a0_ref, b1_ref, b0_ref)


def add_kernel(ids, a_ref, ra_ref, b_ref, rb_ref, ak_ref, as_ref, bk_ref, bs_ref):
    for own, got, keep, send in ((a_ref, ra_ref, ak_ref, as_ref), (b_ref, rb_ref, bk_ref, bs_ref)):
        keep[...] = own[0] + got[0]
        send[...] = own[1] + got[1]


def final_kernel(ids, *refs):
    *in_refs, out_ref = refs
    for i in range(out_ref.shape[0]):
        out_ref[i] = in_refs[2 * i][...] + in_refs[2 * i + 1][...]


def final_cols_kernel(ids, *refs):
    *in_refs, out_ref = refs
    n = in_refs[0].shape[1]
    for i in range(len(in_refs) // 2):
        out_ref[:, i * n:(i + 1) * n] = in_refs[2 * i][...] + in_refs[2 * i + 1][...]


def final_ff_kernel(ids, *refs):
    *in_refs, out_ref = refs
    n = in_refs[0].shape[1]
    for i in range(len(in_refs) // 2):
        unit, c = i // 2, i % 2
        out_ref[:, c, unit * n:(unit + 1) * n] = in_refs[2 * i][...] + in_refs[2 * i + 1][...]


def natural_order(values):
    n = values.shape[1] // SHARD
    blocks = [values[:, s * SHARD:(s + 1) * SHARD] for s in range(n)]
    return jnp.concatenate([blocks[(b % 2) * (n // 2) + b // 2] for b in range(n)], axis=1)


def y_kernel(ids, h_ref, part_ref, recv_ref, y_ref):
    y = (h_ref[...].astype(F32) + (part_ref[...] + recv_ref[...])).astype(BF16)
    y_ref[...] = natural_order(y)


def gx_kernel(ids, gh_ref, x_ref, part_ref, recv_ref, gx_ref):
    normed, inv_std = norm_stats(x_ref[...].astype(F32))
    gx = gh_ref[...] + norm_backward(part_ref[...] + recv_ref[...], normed, inv_std)
    gx_ref[...] = natural_order(gx.astype(BF16))


def swap(value, axis):
    return lax.ppermute(value, axis, SWAP)


def gather(weight, axis):
    return lax.all_gather(weight, ('c', 'y', 'x'), axis=axis, tiled=True)


def layer(x, grad_y, w_qkv, w_out, w_ff, w_down):
    batch, seq, width = x.shape
    heads, head = w_qkv.shape[2:]
    inner = heads * head
    units = w_ff.shape[2]
    tokens = batch * seq
    half = tokens // 2
    z = lax.axis_index('z')
    ids = jnp.stack([z, lax.axis_index('c'), 2 * lax.axis_index('y') + lax.axis_index('x')]).astype(jnp.int32)
    scale = head ** -0.5

    inv_freq = 10000.0 ** (-jnp.arange(0, head, 2, dtype=F32) / head)
    angles = jnp.arange(seq, dtype=F32)[:, None] * inv_freq[None, :]
    cos_tab = jnp.concatenate([jnp.cos(angles), jnp.cos(angles)], axis=1)
    sin_tab = jnp.concatenate([-jnp.sin(angles), jnp.sin(angles)], axis=1)

    br = 128
    per_half = half // br
    steps = tokens // br
    rows = w_ff.shape[0] // steps
    src = lambda i: (((i // per_half + lax.axis_index('z') + 1) % 2) * per_half + i % per_half, 0)
    row = lambda i, s: (i, 0)
    anywhere = pl.BlockSpec(memory_space=pl.ANY)
    wq = w_qkv.reshape(w_qkv.shape[0], 3 * inner)
    wo = w_out.reshape(inner, w_out.shape[2])
    n1, xp, gyp, ff_t, qkv_full, out_full = call(
        head_kernel, (steps,),
        [pl.BlockSpec((br, width), src)] * 2 + [pl.BlockSpec((rows, 2, units), lambda i: (i, 0, 0))] + [anywhere] * 2,
        [pl.BlockSpec((br, width), lambda i: (i, 0))] * 3 + [pl.BlockSpec((2, rows, units), lambda i: (0, i, 0))] + [anywhere] * 2,
        [sds((tokens, width), BF16)] * 3
        + [sds((2, w_ff.shape[0], units), BF16), sds((width, 3 * inner), BF16), sds((2, inner, width // 2), BF16)],
        None, [x.reshape(tokens, width), grad_y.reshape(tokens, width), w_ff, wq, wo], 20 * tokens * width,
        scratch=[pltpu.VMEM(wq.shape, BF16), pltpu.VMEM(wo.shape, BF16), pltpu.SemaphoreType.DMA((4,)),
                 pltpu.SemaphoreType.DMA((2, ROLES)), pltpu.SemaphoreType.DMA((2, ROLES))], collective=0)
    out_z = swap(lax.dynamic_index_in_dim(out_full, lax.axis_index('c'), 0, keepdims=False), 'z')
    out_zc = swap(out_z, 'c')
    ff_full = gather(ff_t, 1)
    down_full = gather(w_down, 1)

    bn = 512
    fixed = lambda *_: (0, 0)
    n_qkv = 3 * inner // bn
    per = n_qkv // 3
    bh = 256
    n_h = inner // bh

    qkv, keep = call(
        functools.partial(qkv_kernel, rotated=2 * per), (n_qkv,),
        [pl.BlockSpec((tokens, width), fixed), pl.BlockSpec((width, bn), lambda j, s: (0, j)),
         pl.BlockSpec((seq, head), fixed), pl.BlockSpec((seq, head), fixed)],
        [pl.BlockSpec((tokens, bn), lambda j, s: (0, j)), pl.BlockSpec((None, tokens, bn), lambda j, s: (j // per, 0, j % per))],
        [sds((tokens, 3 * inner), BF16), sds((3, tokens, inner), BF16)], ids,
        [n1, qkv_full, cos_tab, sin_tab], 2 * tokens * width * 3 * inner)

    def attn_rows(r, old):
        send = not old
        return call(
            functools.partial(attn_kernel, head=head, scale=scale, rows=256, send=send), (n_h,),
            [pl.BlockSpec((half, bh), lambda h, s, p=p: (r, p * n_h + h)) for p in range(3)] + [anywhere] * len(old),
            [pl.BlockSpec((half, bh), lambda h, s: (0, h))] * send + [pl.BlockSpec((half, bh), lambda h, s: (r, h))],
            [sds((half, inner), BF16)] * send + [sds((tokens, inner), BF16)], ids,
            [qkv, qkv, qkv, *old], 4 * half * seq * inner, aliases={4: 0} if old else None)

    def nn(lhs, w, r):
        depth = lhs[0].shape[1]
        return call(
            nn_kernel, (width // bn,),
            [pl.BlockSpec((half, depth), lambda j, s: (r, 0))] * len(lhs) + [pl.BlockSpec((depth * len(lhs), bn), lambda j, s: (0, j))],
            pl.BlockSpec((half, bn), lambda j, s: (0, j)), sds((half, width), F32), ids,
            [*lhs, w], 2 * half * depth * len(lhs) * width)

    o_theirs, attn_o = attn_rows(0, ())
    o_got = swap(o_theirs, 'z')
    (attn_o,) = attn_rows(1, (attn_o,))
    wn = bn // 2
    nw = width // 2 // wn
    part = call(
        out_kernel, (2 * nw,),
        [pl.BlockSpec((half, inner), lambda j, s: (1, 0)), pl.BlockSpec((half, inner), fixed),
         pl.BlockSpec((None, inner, wn), lambda j, s: ((s[1] + j // nw) % 2, 0, j % nw)),
         pl.BlockSpec((inner, wn), lambda j, s: (0, jnp.minimum(j, nw - 1))), pl.BlockSpec((inner, wn), lambda j, s: (0, jnp.maximum(j - nw, 0)))],
        pl.BlockSpec((half, wn), lambda j, s: (0, (s[1] + j // nw) % 2 * nw + j % nw)), sds((half, width), F32), ids,
        [attn_o, o_got, out_full, out_z, out_zc], 4 * half * inner * width)
    mine_rows = lambda i, s: (per_half + i, 0)
    block = pl.BlockSpec((br, width), row)
    hidden, n2_mine = call(
        combine1_kernel, (per_half,), [pl.BlockSpec((br, width), mine_rows), block], [block, block],
        [sds((half, width), BF16)] * 2, ids, [xp, part], 20 * half * width)
    n2_theirs = swap(n2_mine, 'z')

    bf = 256
    hu = units // 2

    def ffn(k):
        nb = hu // bf
        return call(
            ffn_kernel, (nb,),
            [pl.BlockSpec((half, width), fixed)] * 2
            + [pl.BlockSpec((1, width, bf), lambda j, s, c=c: (c, 0, k * nb + j)) for c in range(2)],
            [pl.BlockSpec((tokens, bf), lambda j, s: (0, j))] * 3,
            [sds((tokens, hu), F32)] * 2 + [sds((tokens, hu), BF16)], ids,
            [n2_theirs, n2_mine, ff_full, ff_full], 4 * tokens * width * hu, scratch=[pltpu.VMEM((tokens, width), BF16)])

    up0, gate0, act0 = ffn(0)
    up1, gate1, act1 = ffn(1)
    act0_sib = swap(act0, 'c')
    act1_sib = swap(act1, 'c')
    gyp_sib = swap(gyp, 'c')
    n1_sib = swap(n1, 'c')
    o_sib = swap(attn_o, 'c')
    n2_mine_sib = swap(n2_mine, 'c')
    n2_theirs_sib = swap(n2_theirs, 'c')

    ba = 512

    def two_halves(value):
        return [(value, r) for r in range(2)]

    def source_specs(sources):
        return [pl.BlockSpec((half, width // 2), lambda i, s, r=r: (r, s[1])) for _, r in sources]

    def wgrad_cols(a, a2, sources):
        n = a.shape[1] // ba
        piece = sds((2, a.shape[1] // 2, SHARD), F32)
        lo = pl.BlockSpec((2, ba, SHARD), lambda i, s: (0, jnp.minimum(i, n // 2 - 1), 0))
        hi = pl.BlockSpec((2, ba, SHARD), lambda i, s: (0, jnp.maximum(i - n // 2, 0), 0))
        return call(
            wgrad_cols_kernel, (n,),
            [pl.BlockSpec((tokens, ba), lambda i, s: (0, i))] * 2 + source_specs(sources), [lo, lo, hi, hi], [piece] * 4, ids,
            [a, a2, *(v for v, _ in sources)], 4 * tokens * a.shape[1] * width // 2,
            scratch=[pltpu.VMEM((2 * tokens, width // 2), BF16)])

    def wgrad_rows(sources, b, b2):
        per_b = b.shape[2] // bn
        n = b.shape[0] * per_b
        piece = sds((2, SHARD, n * bn // 2), F32)
        lo = pl.BlockSpec((2, SHARD, bn), lambda i, s: (0, 0, jnp.minimum(i, n // 2 - 1)))
        hi = pl.BlockSpec((2, SHARD, bn), lambda i, s: (0, 0, jnp.maximum(i - n // 2, 0)))
        return call(
            wgrad_rows_kernel, (n,),
            source_specs(sources) + [pl.BlockSpec((1, tokens, bn), lambda i, s: (i // per_b, 0, i % per_b))] * 2,
            [lo, lo, hi, hi], [piece] * 4, ids, [*(v for v, _ in sources), b, b2], 4 * tokens * width // 2 * n * bn,
            scratch=[pltpu.VMEM((width // 2, 2 * tokens), BF16)])

    def sum_plane(pieces):
        a1, a0, b1, b0 = pieces
        got_a = swap(a1, 'x')
        got_b = swap(b1, 'y')
        r, c = a0.shape[1:]
        blk = min(r, 128 if c > 256 else 1024)
        two = pl.BlockSpec((2, blk, c), lambda i, s: (0, i, 0))
        one = pl.BlockSpec((blk, c), row)
        a_keep, a_send, b_keep, b_send = call(
            add_kernel, (r // blk,), [two] * 4, [one] * 4, [sds((r, c), F32)] * 4, ids,
            [a0, got_a, b0, got_b], 8 * r * c)
        return [a_keep, swap(a_send, 'y'), b_keep, swap(b_send, 'x')]

    def final(pairs):
        r, c = pairs[0].shape
        blk = min(r, 128 if c > 256 else 1024)
        return call(
            final_kernel, (r // blk,), [pl.BlockSpec((blk, c), row)] * len(pairs),
            pl.BlockSpec((len(pairs) // 2, blk, c), lambda i, s: (0, i, 0)), sds((len(pairs) // 2, r, c), F32), ids, pairs, 4 * r * c)

    gy_sources = two_halves(gyp) + two_halves(gyp_sib)
    down0 = sum_plane(wgrad_cols(act0, act0_sib, gy_sources))
    down1 = sum_plane(wgrad_cols(act1, act1_sib, gy_sources))
    grad_down = final(down0 + down1).reshape(units, SHARD)

    def dswiglu(k, up, gate):
        nb = hu // bf
        return call(
            dswiglu_kernel, (nb,),
            [pl.BlockSpec((tokens, width), fixed), pl.BlockSpec((bf, width), lambda j, s: (k * nb + j, 0))]
            + [pl.BlockSpec((tokens, bf), lambda j, s: (0, j))] * 2,
            pl.BlockSpec((2, tokens, bf), lambda j, s: (0, 0, j)), sds((2, tokens, hu), BF16), ids,
            [gyp, down_full, up, gate], 2 * tokens * width * hu)

    d0 = dswiglu(0, up0, gate0)
    d1 = dswiglu(1, up1, gate1)
    d0_sib = swap(d0, 'c')
    d1_sib = swap(d1, 'c')

    def grad_n2(r):
        bd = 256
        return call(
            grad_n2_kernel, (width // bd,),
            [pl.BlockSpec((2, half, hu), lambda j, s: (0, r, 0))] * 2 + [pl.BlockSpec((2, bd, units), lambda j, s: (0, j, 0))],
            pl.BlockSpec((half, bd), lambda j, s: (0, j)), sds((half, width), F32), ids,
            [d0, d1, ff_full], 4 * half * width * units)

    gn2_theirs = grad_n2(0)
    gn2_got = swap(gn2_theirs, 'z')
    n2_sources = [(n2_theirs, 0), (n2_mine, 0), (n2_theirs_sib, 0), (n2_mine_sib, 0)]
    ff0 = sum_plane(wgrad_rows(n2_sources, d0, d0_sib))
    ff1 = sum_plane(wgrad_rows(n2_sources, d1, d1_sib))
    br_ff = 32
    grad_ff = call(
        final_ff_kernel, (SHARD // br_ff,), [pl.BlockSpec((br_ff, hu), row)] * 8,
        pl.BlockSpec((br_ff, 2, units), lambda i, s: (i, 0, 0)), sds((SHARD, 2, units), F32), ids, ff0 + ff1, 4 * SHARD * units)
    gn2_mine = grad_n2(1)

    gh, gh_mine = call(
        combine2_kernel, (per_half,),
        [pl.BlockSpec((br, width), mine_rows), block, block, block], [block, block],
        [sds((half, width), F32), sds((half, width), BF16)], ids,
        [gyp, hidden, gn2_mine, gn2_got], 20 * half * width)
    gh_theirs = swap(gh_mine, 'z')
    y_theirs = nn([act0, act1], down_full, 0)
    y_got = swap(y_theirs, 'z')
    y_mine = nn([act0, act1], down_full, 1)

    grad_o = call(
        grad_o_kernel, (inner // bn,),
        [pl.BlockSpec((half, width), fixed)] * 2 + [pl.BlockSpec((2, bn, width // 2), lambda j, s: (0, j, 0))],
        pl.BlockSpec((tokens, bn), lambda j, s: (0, j)), sds((tokens, inner), BF16), ids,
        [gh_theirs, gh_mine, out_full], 2 * tokens * width * inner)
    gh_theirs_sib = swap(gh_theirs, 'c')
    gh_mine_sib = swap(gh_mine, 'c')
    dqkv = call(
        functools.partial(attn_bwd_kernel, head=head, scale=scale, rows=256), (batch, n_h),
        [pl.BlockSpec((seq, bh), lambda b, h, s, p=p: (b, p * n_h + h)) for p in range(3)]
        + [pl.BlockSpec((seq, bh), lambda b, h, s: (b, h)), pl.BlockSpec((3, seq, bh), lambda b, h, s: (0, b, h)),
           pl.BlockSpec((seq, head), fixed), pl.BlockSpec((seq, head), fixed)],
        pl.BlockSpec((3, seq, bh), lambda b, h, s: (0, b, h)), sds((3, tokens, inner), BF16), ids,
        [qkv, qkv, qkv, grad_o, keep, cos_tab, sin_tab], 10 * tokens * seq * inner,
        scratch=[pltpu.VMEM((seq, head), F32)] * 2)
    dqkv_sib = swap(dqkv, 'c')

    def grad_n1(r):
        return call(
            grad_n1_kernel, (width // bn,),
            [pl.BlockSpec((3, half, inner), lambda j, s: (0, r, 0)), pl.BlockSpec((bn, 3 * inner), lambda j, s: (j, 0))],
            pl.BlockSpec((half, bn), lambda j, s: (0, j)), sds((half, width), F32), ids,
            [dqkv, qkv_full], 2 * half * width * 3 * inner)

    gn1_theirs = grad_n1(0)
    gn1_got = swap(gn1_theirs, 'z')
    gh_sources = [(gh_theirs, 0), (gh_mine, 0), (gh_theirs_sib, 0), (gh_mine_sib, 0)]
    out_pairs = sum_plane(wgrad_cols(attn_o, o_sib, gh_sources))
    grad_out = final(out_pairs).reshape(heads, head, SHARD)
    qkv_pairs = sum_plane(wgrad_rows(two_halves(n1) + two_halves(n1_sib), dqkv, dqkv_sib))
    half_cols = 3 * inner // 2
    grad_qkv = call(
        final_cols_kernel, (2,), [pl.BlockSpec((br, half_cols), row)] * 4,
        pl.BlockSpec((br, 3 * inner), row), sds((SHARD, 3 * inner), F32), ids, qkv_pairs, 4 * SHARD * half_cols)
    grad_qkv = grad_qkv.reshape(SHARD, 3, heads, head)
    gn1_mine = grad_n1(1)

    def in_order(theirs, mine):
        both = jnp.where(z == 0, jnp.concatenate([mine, theirs], 0), jnp.concatenate([theirs, mine], 0))
        return both.reshape(batch, seq, width)

    y_own = call(
        y_kernel, (per_half,), [block] * 3, block, sds((half, width), BF16), ids, [hidden, y_mine, y_got], 4 * half * width)
    y_out = in_order(swap(y_own, 'z'), y_own)
    gx_own = call(
        gx_kernel, (per_half,), [block, pl.BlockSpec((br, width), mine_rows), block, block], block,
        sds((half, width), BF16), ids, [gh, xp, gn1_mine, gn1_got], 20 * half * width)
    grad_x = in_order(swap(gx_own, 'z'), gx_own)
    return y_out, grad_x, grad_qkv, grad_out, grad_ff, grad_down


def solution(mesh):
    fine = Mesh(np.asarray(mesh.devices).reshape(2, 2, 2, 2), ('z', 'y', 'x', 'c'))
    fsdp = ('y', 'x', 'c')
    act_spec = P(fsdp, None, None)
    weight_specs = (P(fsdp, None, 'z', None), P('z', None, fsdp), P(fsdp, None, 'z'), P('z', fsdp))
    return jax.shard_map(layer, mesh=fine, in_specs=(act_spec, act_spec) + weight_specs, out_specs=(act_spec, act_spec) + weight_specs, check_vma=False)
```

time: 1300 us -> 1220 us (0.938)
  waiting for transfers between devices: 781 us -> 552 us
  Pallas kernels: 439 us -> 588 us
  starting transfers between devices: 13.3 us -> 35.8 us
  local copies, waits for them, and re-layouts: 32.2 us -> 12.4 us
    reduce_scatter x4 -> x0, waiting for transfers between devices: 311 us -> none  [scatter(): lax.psum_scatter(grad, ('y', 'x'), scatter_dimension=axis, tiled=True)]
    pallas_call x27 -> x37, Pallas kernels: 439 us -> 588 us  [call(): pl.pallas_call(kernel, out_shape=out_shape, grid_spec=pltpu.PrefetchScala...]
    ppermute x18 -> x46, waiting for transfers between devices: 408 us -> 532 us  [swap(): return lax.ppermute(value, axis, SWAP)]
    all_gather x4 -> x2, waiting for transfers between devices: 58.6 us -> 19.5 us  [gather(): return lax.all_gather(weight, ('c', 'y', 'x'), axis=axis, tiled=True)]
    ppermute x18 -> x46, starting transfers between devices: 13 us -> 35.7 us  [swap(): return lax.ppermute(value, axis, SWAP)]
    unnamed x14 -> x28, local copies, waits for them, and re-layouts: 32.2 us -> 10.6 us
  transfers between devices with their start and end apart: 26 -> 48, of which waited for: 13 -> 19; matrix products, arithmetic and copies ran while one was open for 3% -> 1% of each run, Pallas kernels for 27% -> 42%
where the time goes in v2:
time: 1220 us
  Pallas kernels  588 us (48%)
  waiting for transfers between devices  552 us (45%)
  starting transfers between devices  35.8 us (3%)
  between operations  14.5 us (1%)
  other arithmetic  13.7 us (1%)
  local copies, waits for them, and re-layouts  12.4 us (1%)
    pallas_call x37, Pallas kernels, call(): pl.pallas_call(kernel, out_shape=out_shape, grid_spec=pltpu.PrefetchScala...  588 us
    ppermute x46, waiting for transfers between devices, swap(): return lax.ppermute(value, axis, SWAP)  532 us
    ppermute x46, starting transfers between devices, swap(): return lax.ppermute(value, axis, SWAP)  35.7 us
  transfers between devices with their start and end apart: 48, of which 19 were waited for; matrix products, arithmetic and copies ran while one was open for 1% of the time, Pallas kernels for 42%

profile of v2, /device:TPU:0, one launch (start us, length us, event | category | flops | bytes accessed | tf_op | source)
XLA Modules:
  0.0 1215.9 jit_solution(9063115438088604728)
XLA Ops:
  10.1 78.1 %shard_map.109 = (bf16[1024,2048]{1,0:T(8,128)(2,1)}, bf16[1024,2048]{1,0:T(8,128)(2,1)}, bf16[1024,2048]{1,0:T(8,128)(2,1)}, bf16[2,256,4096]{2,1,0:T(8,128)(2,...) custom-call(bf16[1024,2048]{1,0:T(8,128)(2,1)} %bitcast.22, bf16[1024,2048]{1,0:T(8,128)(2,1)} %bitcast.23, ...), custom_call_target="tpu_custom_call" | custom-call | flops 41943040 | bytes 48234496 | tf_op jit(solution)/shard_map/pallas_call | solution.py:53
  95.0 43.8 %collective-permute-done.1.wz_ref = bf16[1024,1024]{1,0:T(8,128)(2,1)} collective-permute-done((bf16[1024,1024]{1,0:T(8,128)(2,1)S(1)}, bf16[1024,1024]{1,0:T(8,128)(2,1)}, u32[]{:S(2)}, u32[]{:S(2)}) %collective-permute-start.1) | collective-permute-done | bytes 2097184 | tf_op jit(solution)/shard_map/ppermute | solution.py:434
  138.8 22.8 %shard_map.110 = (bf16[1024,3072]{1,0:T(8,128)(2,1)}, bf16[3,1024,1024]{2,1,0:T(8,128)(2,1)}) custom-call(s32[3]{0:T(128)} %pad_add_fusion.ids, bf16[1024,2048]{1,0:T(8,128)(2,1)} %get-tuple-element.75.n1_ref.t_ref.m_ref, bf16[2048,3072]{1,0:T(8,128)(2,1)} %get-tuple-element.76.w_ref, f32[512,128]{1,0:T(8,128)} %get-tuple-element.145.cos_ref, ...), custom_call_target="tpu_custom_call" | custom-call | flops 12884901888 | bytes 29884416 | tf_op jit(solution)/shard_map/pallas_call | solution.py:53
  182.8 14.4 %collective-permute-done.got_ref = bf16[512,1024]{1,0:T(8,128)(2,1)S(1)} collective-permute-done((bf16[512,1024]{1,0:T(8,128)(2,1)}, bf16[512,1024]{1,0:T(8,128)(2,1)S(1)}, u32[]{:S(2)}, u32[]{:S(2)}) %collective-permute-start) | collective-permute-done | bytes 1048608 | tf_op jit(solution)/shard_map/ppermute | solution.py:434
  199.6 12.7 %shard_map.113.part_ref = f32[512,2048]{1,0:T(8,128)} custom-call(s32[3]{0:T(128)} %pad_add_fusion.ids, bf16[1024,1024]{1,0:T(8,128)(2,1)} %shard_map.112.o_ref.a_ref, bf16[512,1024]{1,0:T(8,128)(2,1)} %copy-done.12, bf16[2,1024,1024]{2,1,0:T(8,128)(2,1)} %get-tuple-element.80.w_ref, bf16[1024,1024]{1,0:T(8,128)(2,1)} %collective-permute-done.1.wz_ref, ...), custom_call_target="tpu_custom_call" | custom-call | flops 4294967296 | bytes 15728640 | tf_op jit(solution)/shard_map/pallas_call | solution.py:53
  221.1 44.9 %collective-permute-done.3.theirs_ref.t_ref = bf16[512,2048]{1,0:T(8,128)(2,1)S(1)} collective-permute-done((bf16[512,2048]{1,0:T(8,128)(2,1)}, bf16[512,2048]{1,0:T(8,128)(2,1)S(1)}, u32[]{:S(2)}, u32[]{:S(2)}) %collective-permute-start.3) | collective-permute-done | bytes 2097184 | tf_op jit(solution)/shard_map/ppermute | solution.py:434
  267.3 25.0 %shard_map.115 = (f32[1024,2048]{1,0:T(8,128)}, f32[1024,2048]{1,0:T(8,128)}, bf16[1024,2048]{1,0:T(8,128)(2,1)}) custom-call(s32[3]{0:T(128)} %pad_add_fusion.ids, bf16[512,2048]{1,0:T(8,128)(2,1)} %copy-done.1, bf16[512,2048]{1,0:T(8,128)(2,1)} %get-tuple-element.82.mine_ref.m_ref, bf16[2,2048,4096]{2,1,0:T(8,128)(2,1)} %all-gather.3.cloned.1.call-done.wu_ref.wg_ref.w_ref, ...), custom_call_target="tpu_custom_call" | custom-call | flops 17179869184 | bytes 92274688 | tf_op jit(solution)/shard_map/pallas_call | solution.py:53
  292.3 24.9 %shard_map.116 = (f32[1024,2048]{1,0:T(8,128)}, f32[1024,2048]{1,0:T(8,128)}, bf16[1024,2048]{1,0:T(8,128)(2,1)}) custom-call(s32[3]{0:T(128)} %pad_add_fusion.ids, bf16[512,2048]{1,0:T(8,128)(2,1)} %copy-done.1, bf16[512,2048]{1,0:T(8,128)(2,1)} %get-tuple-element.82.mine_ref.m_ref, bf16[2,2048,4096]{2,1,0:T(8,128)(2,1)} %all-gather.3.cloned.1.call-done.wu_ref.wg_ref.w_ref, ...), custom_call_target="tpu_custom_call" | custom-call | flops 17179869184 | bytes 92274688 | tf_op jit(solution)/shard_map/pallas_call | solution.py:53
  317.1 19.5 %all-gather.5.cloned.1.call-done.refs_2_.w_ref = bf16[4096,2048]{1,0:T(8,128)(2,1)} async-done(((bf16[4096,256]{1,0:T(8,128)(2,1)}), bf16[4096,2048]{1,0:T(8,128)(2,1)}) %all-gather.5.cloned.1.call-update) | async-done | bytes 16777232 | tf_op jit(solution)/shard_map/all_gather | solution.py:438
  336.6 14.8 %shard_map.118 = f32[512,2048]{1,0:T(8,128)} custom-call(s32[3]{0:T(128)} %pad_add_fusion.ids, bf16[1024,2048]{1,0:T(8,128)(2,1)} %get-tuple-element.84.refs_0_.a_ref, bf16[1024,2048]{1,0:T(8,128)(2,1)} %get-tuple-element.85.refs_1_.a_ref, bf16[4096,2048]{1,0:T(8,128)(2,1)} %all-gather.5.cloned.1.call-done.refs_2_.w_ref), custom_call_target="tpu_custom_call" | custom-call | flops 8589934592 | bytes 29360128 | tf_op jit(solution)/shard_map/pallas_call | solution.py:53
  352.9 20.2 %shard_map.120.lo_ref.b_ref = bf16[2,1024,2048]{2,1,0:T(8,128)(2,1)} custom-call(s32[3]{0:T(128)} %pad_add_fusion.ids, bf16[1024,2048]{1,0:T(8,128)(2,1)} %get-tuple-element.86.gy_ref.t_ref.m_ref, bf16[4096,2048]{1,0:T(8,128)(2,1)} %all-gather.5.cloned.1.call-done.refs_2_.w_ref, f32[1024,2048]{1,0:T(8,128)} %get-tuple-element.87.u_ref, ...), custom_call_target="tpu_custom_call" | custom-call | flops 8589934592 | bytes 46137344 | tf_op jit(solution)/shard_map/pallas_call | solution.py:53
  373.0 19.6 %shard_map.121.hi_ref.b_ref = bf16[2,1024,2048]{2,1,0:T(8,128)(2,1)} custom-call(s32[3]{0:T(128)} %pad_add_fusion.ids, bf16[1024,2048]{1,0:T(8,128)(2,1)} %get-tuple-element.86.gy_ref.t_ref.m_ref, bf16[4096,2048]{1,0:T(8,128)(2,1)} %all-gather.5.cloned.1.call-done.refs_2_.w_ref, f32[1024,2048]{1,0:T(8,128)} %get-tuple-element.89.u_ref, ...), custom_call_target="tpu_custom_call" | custom-call | flops 8589934592 | bytes 46137344 | tf_op jit(solution)/shard_map/pallas_call | solution.py:53
  392.6 25.5 %shard_map.123 = f32[512,2048]{1,0:T(8,128)} custom-call(s32[3]{0:T(128)} %pad_add_fusion.ids, bf16[2,1024,2048]{2,1,0:T(8,128)(2,1)} %shard_map.120.lo_ref.b_ref, bf16[2,1024,2048]{2,1,0:T(8,128)(2,1)} %shard_map.121.hi_ref.b_ref, bf16[2,2048,4096]{2,1,0:T(8,128)(2,1)} %all-gather.3.cloned.1.call-done.wu_ref.wg_ref.w_ref), custom_call_target="tpu_custom_call" | custom-call | flops 17179869184 | bytes 54525952 | tf_op jit(solution)/shard_map/pallas_call | solution.py:53
  419.2 25.9 %collective-permute-done.4.recv_ref = f32[512,2048]{1,0:T(8,128)} collective-permute-done((f32[512,2048]{1,0:T(8,128)}, f32[512,2048]{1,0:T(8,128)}, u32[]{:S(2)}, u32[]{:S(2)}) %collective-permute-start.4) | collective-permute-done | bytes 4194336 | tf_op jit(solution)/shard_map/ppermute | solution.py:434
  445.2 25.4 %shard_map.122.part_ref = f32[512,2048]{1,0:T(8,128)} custom-call(s32[3]{0:T(128)} %pad_add_fusion.ids, bf16[2,1024,2048]{2,1,0:T(8,128)(2,1)} %shard_map.120.lo_ref.b_ref, bf16[2,1024,2048]{2,1,0:T(8,128)(2,1)} %shard_map.121.hi_ref.b_ref, bf16[2,2048,4096]{2,1,0:T(8,128)(2,1)} %all-gather.3.cloned.1.call-done.wu_ref.wg_ref.w_ref), custom_call_target="tpu_custom_call" | custom-call | flops 17179869184 | bytes 54525952 | tf_op jit(solution)/shard_map/pallas_call | solution.py:53
  470.5 14.8 %shard_map.117.part_ref = f32[512,2048]{1,0:T(8,128)} custom-call(s32[3]{0:T(128)} %pad_add_fusion.ids, bf16[1024,2048]{1,0:T(8,128)(2,1)} %get-tuple-element.84.refs_0_.a_ref, bf16[1024,2048]{1,0:T(8,128)(2,1)} %get-tuple-element.85.refs_1_.a_ref, bf16[4096,2048]{1,0:T(8,128)(2,1)} %all-gather.5.cloned.1.call-done.refs_2_.w_ref), custom_call_target="tpu_custom_call" | custom-call | flops 8589934592 | bytes 29360128 | tf_op jit(solution)/shard_map/pallas_call | solution.py:53
  491.7 42.6 %collective-permute-done.6.recv_ref = f32[512,2048]{1,0:T(8,128)} collective-permute-done((f32[512,2048]{1,0:T(8,128)}, f32[512,2048]{1,0:T(8,128)}, u32[]{:S(2)}, u32[]{:S(2)}) %collective-permute-start.6) | collective-permute-done | bytes 4194336 | tf_op jit(solution)/shard_map/ppermute | solution.py:434
  546.1 16.5 %shard_map.141 = (f32[2,1024,256]{2,1,0:T(8,128)}, f32[2,1024,256]{2,1,0:T(8,128)}, f32[2,1024,256]{2,1,0:T(8,128)}, f32[2,1024,256]{2,1,0:T(8,128)}) custom-call(s32[3]{0:T(128)} %pad_add_fusion.ids, bf16[1024,2048]{1,0:T(8,128)(2,1)} %get-tuple-element.84.refs_0_.a_ref, bf16[1024,2048]{1,0:T(8,128)(2,1)} %collective-permute-done.35.a2_ref, ...), custom_call_target="tpu_custom_call" | custom-call | flops 8589934592 | bytes 33554432 | tf_op jit(solution)/shard_map/pallas_call | solution.py:53
  562.6 20.5 %collective-permute-done.5 = bf16[512,2048]{1,0:T(8,128)(2,1)} collective-permute-done((bf16[512,2048]{1,0:T(8,128)(2,1)}, bf16[512,2048]{1,0:T(8,128)(2,1)}, u32[]{:S(2)}, u32[]{:S(2)}) %collective-permute-start.5) | collective-permute-done | bytes 2097184 | tf_op jit(solution)/shard_map/ppermute | solution.py:434
  584.6 41.8 %collective-permute-done.7.theirs_ref.t_ref = bf16[512,2048]{1,0:T(8,128)(2,1)S(1)} collective-permute-done((bf16[512,2048]{1,0:T(8,128)(2,1)}, bf16[512,2048]{1,0:T(8,128)(2,1)S(1)}, u32[]{:S(2)}, u32[]{:S(2)}) %collective-permute-start.7) | collective-permute-done | bytes 2097184 | tf_op jit(solution)/shard_map/ppermute | solution.py:434
  626.8 16.9 %shard_map.143 = (f32[2,1024,256]{2,1,0:T(8,128)}, f32[2,1024,256]{2,1,0:T(8,128)}, f32[2,1024,256]{2,1,0:T(8,128)}, f32[2,1024,256]{2,1,0:T(8,128)}) custom-call(s32[3]{0:T(128)} %pad_add_fusion.ids, bf16[1024,2048]{1,0:T(8,128)(2,1)} %get-tuple-element.85.refs_1_.a_ref, bf16[1024,2048]{1,0:T(8,128)(2,1)} %collective-permute-done.41.a2_ref, ...), custom_call_target="tpu_custom_call" | custom-call | flops 8589934592 | bytes 33554432 | tf_op jit(solution)/shard_map/pallas_call | solution.py:53
  646.8 28.4 %collective-permute-done.38.rb_ref = f32[2,1024,256]{2,1,0:T(8,128)} collective-permute-done((f32[2,1024,256]{2,1,0:T(8,128)}, f32[2,1024,256]{2,1,0:T(8,128)}, u32[]{:S(2)}, u32[]{:S(2)}) %collective-permute-start.38) | collective-permute-done | bytes 2097184 | tf_op jit(solution)/shard_map/ppermute | solution.py:434
  684.5 26.4 %shard_map.126.d_ref.b_ref = bf16[3,1024,1024]{2,1,0:T(8,128)(2,1)} custom-call(s32[3]{0:T(128)} %pad_add_fusion.ids, bf16[1024,3072]{1,0:T(8,128)(2,1)} %get-tuple-element.77.q_ref.k_ref.v_ref, bf16[1024,3072]{1,0:T(8,128)(2,1)} %get-tuple-element.77.q_ref.k_ref.v_ref, bf16[1024,3072]{1,0:T(8,128)(2,1)} %get-tuple-element.77.q_ref.k_ref.v_ref, ...), custom_call_target="tpu_custom_call" | custom-call | flops 5368709120 | bytes 34078720 | tf_op jit(solution)/shard_map/pallas_call | solution.py:53
  726.1 12.4 %shard_map.128 = f32[512,2048]{1,0:T(8,128)} custom-call(s32[3]{0:T(128)} %pad_add_fusion.ids, bf16[3,1024,1024]{2,1,0:T(8,128)(2,1)} %shard_map.126.d_ref.b_ref, bf16[2048,3072]{1,0:T(8,128)(2,1)} %get-tuple-element.76.w_ref), custom_call_target="tpu_custom_call" | custom-call | flops 6442450944 | bytes 23068672 | tf_op jit(solution)/shard_map/pallas_call | solution.py:53
  753.2 27.2 %shard_map.136 = (f32[2,256,2048]{2,1,0:T(8,128)}, f32[2,256,2048]{2,1,0:T(8,128)}, f32[2,256,2048]{2,1,0:T(8,128)}, f32[2,256,2048]{2,1,0:T(8,128)}) custom-call(s32[3]{0:T(128)} %pad_add_fusion.ids, bf16[512,2048]{1,0:T(8,128)(2,1)} %copy-done.1, bf16[512,2048]{1,0:T(8,128)(2,1)} %get-tuple-element.82.mine_ref.m_ref, ...), custom_call_target="tpu_custom_call" | custom-call | flops 17179869184 | bytes 41943040 | tf_op jit(solution)/shard_map/pallas_call | solution.py:53
  783.1 16.9 %collective-permute-done.19.ra_ref = f32[2,512,256]{2,1,0:T(8,128)} collective-permute-done((f32[2,512,256]{2,1,0:T(8,128)}, f32[2,512,256]{2,1,0:T(8,128)}, u32[]{:S(2)}, u32[]{:S(2)}) %collective-permute-start.19) | collective-permute-done | bytes 1048608 | tf_op jit(solution)/shard_map/ppermute | solution.py:434
  800.5 27.1 %shard_map.138 = (f32[2,256,2048]{2,1,0:T(8,128)}, f32[2,256,2048]{2,1,0:T(8,128)}, f32[2,256,2048]{2,1,0:T(8,128)}, f32[2,256,2048]{2,1,0:T(8,128)}) custom-call(s32[3]{0:T(128)} %pad_add_fusion.ids, bf16[512,2048]{1,0:T(8,128)(2,1)} %copy-done.1, bf16[512,2048]{1,0:T(8,128)(2,1)} %get-tuple-element.82.mine_ref.m_ref, ...), custom_call_target="tpu_custom_call" | custom-call | flops 17179869184 | bytes 41943040 | tf_op jit(solution)/shard_map/pallas_call | solution.py:53
  827.6 68.0 %collective-permute-done.20.rb_ref = f32[2,512,256]{2,1,0:T(8,128)S(1)} collective-permute-done((f32[2,512,256]{2,1,0:T(8,128)}, f32[2,512,256]{2,1,0:T(8,128)S(1)}, u32[]{:S(2)}, u32[]{:S(2)}) %collective-permute-start.20) | collective-permute-done | bytes 1048608 | tf_op jit(solution)/shard_map/ppermute | solution.py:434
  897.7 22.1 %shard_map.130 = (f32[2,256,1536]{2,1,0:T(8,128)}, f32[2,256,1536]{2,1,0:T(8,128)}, f32[2,256,1536]{2,1,0:T(8,128)}, f32[2,256,1536]{2,1,0:T(8,128)}) custom-call(s32[3]{0:T(128)} %pad_add_fusion.ids, bf16[1024,2048]{1,0:T(8,128)(2,1)} %get-tuple-element.75.n1_ref.t_ref.m_ref, bf16[1024,2048]{1,0:T(8,128)(2,1)} %get-tuple-element.75.n1_ref.t_ref.m_ref, ...), custom_call_target="tpu_custom_call" | custom-call | flops 12884901888 | bytes 41943040 | tf_op jit(solution)/shard_map/pallas_call | solution.py:53
  958.1 108.1 %collective-permute-done.21.refs_1_ = f32[512,256]{1,0:T(8,128)S(1)} collective-permute-done((f32[512,256]{1,0:T(8,128)}, f32[512,256]{1,0:T(8,128)S(1)}, u32[]{:S(2)}, u32[]{:S(2)}) %collective-permute-start.21) | collective-permute-done | bytes 524320 | tf_op jit(solution)/shard_map/ppermute | solution.py:434
  1090.2 18.9 %collective-permute-done.9 = bf16[512,2048]{1,0:T(8,128)(2,1)} collective-permute-done((bf16[512,2048]{1,0:T(8,128)(2,1)}, bf16[512,2048]{1,0:T(8,128)(2,1)}, u32[]{:S(2)}, u32[]{:S(2)}) %collective-permute-start.9) | collective-permute-done | bytes 2097184 | tf_op jit(solution)/shard_map/ppermute | solution.py:434
  1136.5 23.6 %collective-permute-done.33.refs_5_ = f32[256,2048]{1,0:T(8,128)} collective-permute-done((f32[256,2048]{1,0:T(8,128)}, f32[256,2048]{1,0:T(8,128)}, u32[]{:S(2)}, u32[]{:S(2)}) %collective-permute-start.33) | collective-permute-done | bytes 2097184 | tf_op jit(solution)/shard_map/ppermute | solution.py:434
  (138 shorter events, 252.0 us)
Async XLA Ops:
  7.2 258.8 %all-gather.3.cloned.1.call-start = ((), (), s32[]{:S(2)}) async-start(), calls=%async_computation | async-start | bytes 37748736 | tf_op jit(solution)/shard_map/all_gather | solution.py:438
  88.2 248.4 %all-gather.5.cloned.1.call-start = ((), (), s32[]{:S(2)}) async-start(), calls=%async_computation.1 | async-start | bytes 18874368 | tf_op jit(solution)/shard_map/all_gather | solution.py:438
  220.1 198.6 %collective-permute-start.10 = (bf16[1024,2048]{1,0:T(8,128)(2,1)}, bf16[1024,2048]{1,0:T(8,128)(2,1)}, u32[]{:S(2)}, u32[]{:S(2)}) collective-permute-start(bf16[1024,2048]{1,0:T(8,128)(2,1)} %get-tuple-element.75.n1_ref.t_ref.m_ref), channel_id=1, source_target_pairs={{0,1},{1,0},{2,3},{3,2},{4,5},{5,4},{6,7},{7,6},{8,9},{9,8},{10,11... | collective-permute-start | bytes 12582920 | tf_op jit(solution)/shard_map/ppermute | solution.py:434
  220.1 198.0 %collective-permute-start.16 = (bf16[1024,1024]{1,0:T(8,128)(2,1)}, bf16[1024,1024]{1,0:T(8,128)(2,1)}, u32[]{:S(2)}, u32[]{:S(2)}) collective-permute-start(bf16[1024,1024]{1,0:T(8,128)(2,1)} %shard_map.112.o_ref.a_ref), channel_id=1, source_target_pairs={{0,1},{1,0},{2,3},{3,2},{4,5},{5,4},{6,7},{7,6},{8,9},{9,8},{10,11... | collective-permute-start | bytes 6291464 | tf_op jit(solution)/shard_map/ppermute | solution.py:434
  220.6 198.1 %collective-permute-start.36 = (bf16[1024,2048]{1,0:T(8,128)(2,1)}, bf16[1024,2048]{1,0:T(8,128)(2,1)}, u32[]{:S(2)}, u32[]{:S(2)}) collective-permute-start(bf16[1024,2048]{1,0:T(8,128)(2,1)} %get-tuple-element.86.gy_ref.t_ref.m_ref), channel_id=1, source_target_pairs={{0,1},{1,0},{2,3},{3,2},{4,5},{5,4},{6,7},{7,6},{8,9},{9,8},{10,11... | collective-permute-start | bytes 12582920 | tf_op jit(solution)/shard_map/ppermute | solution.py:434
  220.6 198.6 %collective-permute-start.24 = (bf16[512,2048]{1,0:T(8,128)(2,1)}, bf16[512,2048]{1,0:T(8,128)(2,1)}, u32[]{:S(2)}, u32[]{:S(2)}) collective-permute-start(bf16[512,2048]{1,0:T(8,128)(2,1)} %get-tuple-element.82.mine_ref.m_ref), channel_id=1, source_target_pairs={{0,1},{1,0},{2,3},{3,2},{4,5},{5,4},{6,7},{7,6},{8,9},{9,8},{10,11... | collective-permute-start | bytes 6291464 | tf_op jit(solution)/shard_map/ppermute | solution.py:434
  351.4 93.8 %collective-permute-start.4 = (f32[512,2048]{1,0:T(8,128)}, f32[512,2048]{1,0:T(8,128)}, u32[]{:S(2)}, u32[]{:S(2)}) collective-permute-start(f32[512,2048]{1,0:T(8,128)} %shard_map.118), channel_id=1, source_target_pairs={{0,8},{8,0},{1,9},{9,1},{2,10},{10,2},{3,11},{11,3},{4,12},{12,4},... | collective-permute-start | bytes 12582920 | tf_op jit(solution)/shard_map/ppermute | solution.py:434
  418.1 116.2 %collective-permute-start.6 = (f32[512,2048]{1,0:T(8,128)}, f32[512,2048]{1,0:T(8,128)}, u32[]{:S(2)}, u32[]{:S(2)}) collective-permute-start(f32[512,2048]{1,0:T(8,128)} %shard_map.123), channel_id=1, source_target_pairs={{0,8},{8,0},{1,9},{9,1},{2,10},{10,2},{3,11},{11,3},{4,12},{12,4},... | collective-permute-start | bytes 12582920 | tf_op jit(solution)/shard_map/ppermute | solution.py:434
  418.7 126.9 %collective-permute-start.35 = (bf16[1024,2048]{1,0:T(8,128)(2,1)}, bf16[1024,2048]{1,0:T(8,128)(2,1)}, u32[]{:S(2)}, u32[]{:S(2)}) collective-permute-start(bf16[1024,2048]{1,0:T(8,128)(2,1)} %get-tuple-element.84.refs_0_.a_ref), channel_id=1, source_target_pairs={{0,1},{1,0},{2,3},{3,2},{4,5},{5,4},{6,7},{7,6},{8,9},{9,8},{10,11... | collective-permute-start | bytes 12582920 | tf_op jit(solution)/shard_map/ppermute | solution.py:434
  418.7 126.9 %collective-permute-start.41 = (bf16[1024,2048]{1,0:T(8,128)(2,1)}, bf16[1024,2048]{1,0:T(8,128)(2,1)}, u32[]{:S(2)}, u32[]{:S(2)}) collective-permute-start(bf16[1024,2048]{1,0:T(8,128)(2,1)} %get-tuple-element.85.refs_1_.a_ref), channel_id=1, source_target_pairs={{0,1},{1,0},{2,3},{3,2},{4,5},{5,4},{6,7},{7,6},{8,9},{9,8},{10,11... | collective-permute-start | bytes 12582920 | tf_op jit(solution)/shard_map/ppermute | solution.py:434
  419.2 125.8 %collective-permute-start.23 = (bf16[512,2048]{1,0:T(8,128)(2,1)S(1)}, bf16[512,2048]{1,0:T(8,128)(2,1)}, u32[]{:S(2)}, u32[]{:S(2)}) collective-permute-start(bf16[512,2048]{1,0:T(8,128)(2,1)S(1)} %copy-done.2), channel_id=1, source_target_pairs={{0,1},{1,0},{2,3},{3,2},{4,5},{5,4},{6,7},{7,6},{8,9},{9,8},{10,11... | collective-permute-start | bytes 6291464 | tf_op jit(solution)/shard_map/ppermute | solution.py:434
  445.2 306.5 %collective-permute-start.25 = (bf16[2,1024,2048]{2,1,0:T(8,128)(2,1)}, bf16[2,1024,2048]{2,1,0:T(8,128)(2,1)}, u32[]{:S(2)}, u32[]{:S(2)}) collective-permute-start(bf16[2,1024,2048]{2,1,0:T(8,128)(2,1)} %shard_map.120.lo_ref.b_ref), channel_id=1, source_target_pairs={{0,1},{1,0},{2,3},{3,2},{4,5},{5,4},{6,7},{7,6},{8,9},{9,8},{10,11... | collective-permute-start | bytes 25165832 | tf_op jit(solution)/shard_map/ppermute | solution.py:434
  545.0 81.4 %collective-permute-start.7 = (bf16[512,2048]{1,0:T(8,128)(2,1)}, bf16[512,2048]{1,0:T(8,128)(2,1)S(1)}, u32[]{:S(2)}, u32[]{:S(2)}) collective-permute-start(bf16[512,2048]{1,0:T(8,128)(2,1)} %get-tuple-element.92.mine_ref.m_ref), channel_id=1, source_target_pairs={{0,8},{8,0},{1,9},{9,1},{2,10},{10,2},{3,11},{11,3},{4,12},{12,4},... | collective-permute-start | bytes 6291464 | tf_op jit(solution)/shard_map/ppermute | solution.py:434
  545.6 236.9 %collective-permute-start.30 = (bf16[2,1024,2048]{2,1,0:T(8,128)(2,1)}, bf16[2,1024,2048]{2,1,0:T(8,128)(2,1)}, u32[]{:S(2)}, u32[]{:S(2)}) collective-permute-start(bf16[2,1024,2048]{2,1,0:T(8,128)(2,1)} %shard_map.121.hi_ref.b_ref), channel_id=1, source_target_pairs={{0,1},{1,0},{2,3},{3,2},{4,5},{5,4},{6,7},{7,6},{8,9},{9,8},{10,11... | collective-permute-start | bytes 25165832 | tf_op jit(solution)/shard_map/ppermute | solution.py:434
  545.6 98.0 %collective-permute-start.18 = (bf16[512,2048]{1,0:T(8,128)(2,1)}, bf16[512,2048]{1,0:T(8,128)(2,1)}, u32[]{:S(2)}, u32[]{:S(2)}) collective-permute-start(bf16[512,2048]{1,0:T(8,128)(2,1)} %get-tuple-element.92.mine_ref.m_ref), channel_id=1, source_target_pairs={{0,1},{1,0},{2,3},{3,2},{4,5},{5,4},{6,7},{7,6},{8,9},{9,8},{10,11... | collective-permute-start | bytes 6291464 | tf_op jit(solution)/shard_map/ppermute | solution.py:434
  583.1 62.2 %collective-permute-start.37 = (f32[2,1024,256]{2,1,0:T(8,128)}, f32[2,1024,256]{2,1,0:T(8,128)}, u32[]{:S(2)}, u32[]{:S(2)}) collective-permute-start(f32[2,1024,256]{2,1,0:T(8,128)} %get-tuple-element.127), channel_id=1, source_target_pairs={{0,2},{2,0},{1,3},{3,1},{4,6},{6,4},{5,7},{7,5},{8,10},{10,8},{9,1... | collective-permute-start | bytes 6291464 | tf_op jit(solution)/shard_map/ppermute | solution.py:434
  643.7 67.2 %collective-permute-start.42 = (f32[2,1024,256]{2,1,0:T(8,128)}, f32[2,1024,256]{2,1,0:T(8,128)S(1)}, u32[]{:S(2)}, u32[]{:S(2)}) collective-permute-start(f32[2,1024,256]{2,1,0:T(8,128)} %get-tuple-element.135), channel_id=1, source_target_pairs={{0,2},{2,0},{1,3},{3,1},{4,6},{6,4},{5,7},{7,5},{8,10},{10,8},{9,1... | collective-permute-start | bytes 6291464 | tf_op jit(solution)/shard_map/ppermute | solution.py:434
  645.4 72.5 %collective-permute-start.43 = (f32[2,1024,256]{2,1,0:T(8,128)}, f32[2,1024,256]{2,1,0:T(8,128)}, u32[]{:S(2)}, u32[]{:S(2)}) collective-permute-start(f32[2,1024,256]{2,1,0:T(8,128)} %get-tuple-element.137), channel_id=1, source_target_pairs={{0,4},{4,0},{1,5},{5,1},{2,6},{6,2},{3,7},{7,3},{8,12},{12,8},{9,1... | collective-permute-start | bytes 6291464 | tf_op jit(solution)/shard_map/ppermute | solution.py:434
  710.9 186.2 %collective-permute-start.11 = (bf16[3,1024,1024]{2,1,0:T(8,128)(2,1)}, bf16[3,1024,1024]{2,1,0:T(8,128)(2,1)}, u32[]{:S(2)}, u32[]{:S(2)}) collective-permute-start(bf16[3,1024,1024]{2,1,0:T(8,128)(2,1)} %shard_map.126.d_ref.b_ref), channel_id=1, source_target_pairs={{0,1},{1,0},{2,3},{3,2},{4,5},{5,4},{6,7},{7,6},{8,9},{9,8},{10,11... | collective-permute-start | bytes 18874376 | tf_op jit(solution)/shard_map/ppermute | solution.py:434
  780.4 139.3 %collective-permute-start.8 = (f32[512,2048]{1,0:T(8,128)}, f32[512,2048]{1,0:T(8,128)}, u32[]{:S(2)}, u32[]{:S(2)}) collective-permute-start(f32[512,2048]{1,0:T(8,128)} %shard_map.128), channel_id=1, source_target_pairs={{0,8},{8,0},{1,9},{9,1},{2,10},{10,2},{3,11},{11,3},{4,12},{12,4},... | collective-permute-start | bytes 12582920 | tf_op jit(solution)/shard_map/ppermute | solution.py:434
  781.9 138.4 %collective-permute-start.26 = (f32[2,256,2048]{2,1,0:T(8,128)}, f32[2,256,2048]{2,1,0:T(8,128)}, u32[]{:S(2)}, u32[]{:S(2)}) collective-permute-start(f32[2,256,2048]{2,1,0:T(8,128)} %get-tuple-element.111), channel_id=1, source_target_pairs={{0,2},{2,0},{1,3},{3,1},{4,6},{6,4},{5,7},{7,5},{8,10},{10,8},{9,1... | collective-permute-start | bytes 12582920 | tf_op jit(solution)/shard_map/ppermute | solution.py:434
  782.5 143.5 %collective-permute-start.27 = (f32[2,256,2048]{2,1,0:T(8,128)}, f32[2,256,2048]{2,1,0:T(8,128)}, u32[]{:S(2)}, u32[]{:S(2)}) collective-permute-start(f32[2,256,2048]{2,1,0:T(8,128)} %get-tuple-element.113), channel_id=1, source_target_pairs={{0,4},{4,0},{1,5},{5,1},{2,6},{6,2},{3,7},{7,3},{8,12},{12,8},{9,1... | collective-permute-start | bytes 12582920 | tf_op jit(solution)/shard_map/ppermute | solution.py:434
  799.9 95.7 %collective-permute-start.20 = (f32[2,512,256]{2,1,0:T(8,128)}, f32[2,512,256]{2,1,0:T(8,128)S(1)}, u32[]{:S(2)}, u32[]{:S(2)}) collective-permute-start(f32[2,512,256]{2,1,0:T(8,128)} %get-tuple-element.105), channel_id=1, source_target_pairs={{0,4},{4,0},{1,5},{5,1},{2,6},{6,2},{3,7},{7,3},{8,12},{12,8},{9,1... | collective-permute-start | bytes 3145736 | tf_op jit(solution)/shard_map/ppermute | solution.py:434
  895.6 170.6 %collective-permute-start.31 = (f32[2,256,2048]{2,1,0:T(8,128)}, f32[2,256,2048]{2,1,0:T(8,128)}, u32[]{:S(2)}, u32[]{:S(2)}) collective-permute-start(f32[2,256,2048]{2,1,0:T(8,128)} %get-tuple-element.119), channel_id=1, source_target_pairs={{0,2},{2,0},{1,3},{3,1},{4,6},{6,4},{5,7},{7,5},{8,10},{10,8},{9,1... | collective-permute-start | bytes 12582920 | tf_op jit(solution)/shard_map/ppermute | solution.py:434
  897.1 169.8 %collective-permute-start.32 = (f32[2,256,2048]{2,1,0:T(8,128)}, f32[2,256,2048]{2,1,0:T(8,128)}, u32[]{:S(2)}, u32[]{:S(2)}) collective-permute-start(f32[2,256,2048]{2,1,0:T(8,128)} %get-tuple-element.121), channel_id=1, source_target_pairs={{0,4},{4,0},{1,5},{5,1},{2,6},{6,2},{3,7},{7,3},{8,12},{12,8},{9,1... | collective-permute-start | bytes 12582920 | tf_op jit(solution)/shard_map/ppermute | solution.py:434
  919.8 159.7 %collective-permute-start.12 = (f32[2,256,1536]{2,1,0:T(8,128)}, f32[2,256,1536]{2,1,0:T(8,128)S(1)}, u32[]{:S(2)}, u32[]{:S(2)}) collective-permute-start(f32[2,256,1536]{2,1,0:T(8,128)} %get-tuple-element.95), channel_id=1, source_target_pairs={{0,2},{2,0},{1,3},{3,1},{4,6},{6,4},{5,7},{7,5},{8,10},{10,8},{9,1... | collective-permute-start | bytes 9437192 | tf_op jit(solution)/shard_map/ppermute | solution.py:434
  920.4 160.5 %collective-permute-start.13 = (f32[2,256,1536]{2,1,0:T(8,128)}, f32[2,256,1536]{2,1,0:T(8,128)}, u32[]{:S(2)}, u32[]{:S(2)}) collective-permute-start(f32[2,256,1536]{2,1,0:T(8,128)} %get-tuple-element.97), channel_id=1, source_target_pairs={{0,4},{4,0},{1,5},{5,1},{2,6},{6,2},{3,7},{7,3},{8,12},{12,8},{9,1... | collective-permute-start | bytes 9437192 | tf_op jit(solution)/shard_map/ppermute | solution.py:434
  926.0 140.2 %collective-permute-start.21 = (f32[512,256]{1,0:T(8,128)}, f32[512,256]{1,0:T(8,128)S(1)}, u32[]{:S(2)}, u32[]{:S(2)}) collective-permute-start(f32[512,256]{1,0:T(8,128)} %get-tuple-element.107), channel_id=1, source_target_pairs={{0,4},{4,0},{1,5},{5,1},{2,6},{6,2},{3,7},{7,3},{8,12},{12,8},{9,1... | collective-permute-start | bytes 1572872 | tf_op jit(solution)/shard_map/ppermute | solution.py:434
  1079.4 80.6 %collective-permute-start.33 = (f32[256,2048]{1,0:T(8,128)}, f32[256,2048]{1,0:T(8,128)}, u32[]{:S(2)}, u32[]{:S(2)}) collective-permute-start(f32[256,2048]{1,0:T(8,128)} %get-tuple-element.123), channel_id=1, source_target_pairs={{0,4},{4,0},{1,5},{5,1},{2,6},{6,2},{3,7},{7,3},{8,12},{12,8},{9,1... | collective-permute-start | bytes 6291464 | tf_op jit(solution)/shard_map/ppermute | solution.py:434
  1080.9 90.9 %collective-permute-start.34 = (f32[256,2048]{1,0:T(8,128)}, f32[256,2048]{1,0:T(8,128)}, u32[]{:S(2)}, u32[]{:S(2)}) collective-permute-start(f32[256,2048]{1,0:T(8,128)} %get-tuple-element.125), channel_id=1, source_target_pairs={{0,2},{2,0},{1,3},{3,1},{4,6},{6,4},{5,7},{7,5},{8,10},{10,8},{9,1... | collective-permute-start | bytes 6291464 | tf_op jit(solution)/shard_map/ppermute | solution.py:434
  1109.1 79.9 %collective-permute-start.14 = (f32[256,1536]{1,0:T(8,128)}, f32[256,1536]{1,0:T(8,128)}, u32[]{:S(2)}, u32[]{:S(2)}) collective-permute-start(f32[256,1536]{1,0:T(8,128)} %get-tuple-element.99), channel_id=1, source_target_pairs={{0,4},{4,0},{1,5},{5,1},{2,6},{6,2},{3,7},{7,3},{8,12},{12,8},{9,1... | collective-permute-start | bytes 4718600 | tf_op jit(solution)/shard_map/ppermute | solution.py:434
  1115.1 84.9 %collective-permute-start.15 = (f32[256,1536]{1,0:T(8,128)}, f32[256,1536]{1,0:T(8,128)}, u32[]{:S(2)}, u32[]{:S(2)}) collective-permute-start(f32[256,1536]{1,0:T(8,128)} %get-tuple-element.101), channel_id=1, source_target_pairs={{0,2},{2,0},{1,3},{3,1},{4,6},{6,4},{5,7},{7,5},{8,10},{10,8},{9,1... | collective-permute-start | bytes 4718600 | tf_op jit(solution)/shard_map/ppermute | solution.py:434
  (29 other events, 889.8 us)
Sparse Core Ops, SparseCore 0:
  88.4 157.0 all-gather.2
  247.3 89.2 all-gather.4
